TPU v7x, 32 devices: a whole 2x2x4 slice. The times are simulated.
32 devices in a mesh: lat: 4 (over y, x), lon: 8 (over z, core).
Axes of the slice: x: 2, y: 2, z: 4, core: 2. Of those that a mesh axis runs over, the one named last changes fastest.
Arguments:
- activations: bfloat16 [4, 16, 720, 512], P(None, 'lat', 'lon'), may hold values from -48 to 48
- upstream: bfloat16 [4, 16, 720, 512], P(None, 'lat', 'lon'), may hold values from -6 to 6
- master: float32 [512, 9, 512], P(('lat', 'lon')), may hold values from -0.09375 to 0.09375
- moment_one: float32 [512, 9, 512], P(('lat', 'lon')), may hold values from -2.5 to 2.5
- moment_two: float32 [512, 9, 512], P(('lat', 'lon')), may hold values from 0.01 to 1
Outputs:
- input_grad: bfloat16 [4, 16, 720, 512], P(None, 'lat', 'lon')
- new_weights: bfloat16 [512, 9, 512], replicated
- new_master: float32 [512, 9, 512], P(('lat', 'lon'))
- new_moment_one: float32 [512, 9, 512], P(('lat', 'lon'))
- new_moment_two: float32 [512, 9, 512], P(('lat', 'lon'))
- clipped_grad: float32 [512, 9, 512], P(('lat', 'lon'))
All inputs are finite; a program needn't handle non-finite values.
Results may differ from a plain program's by a relative error of at most 0.0049.
Values may be sent and summed in bfloat16 or wider, within the bound.
A program may use at most 128 MiB of HBM per device.

v0:
```python
import functools
import math

import jax
import jax.numpy as jnp
from jax import lax
from jax.experimental import pallas as pl
from jax.experimental.pallas import tpu as pltpu
from jax.sharding import PartitionSpec as P

MESH = pl.DeviceIdType.MESH

CIN = 512
COUT = 512
TAPS = 9


learn_rate = 0.01
beta_one = 0.9
beta_two = 0.999
adam_eps = 1e-08
decay_rate = 0.1
step_count = 10.0
norm_eps = 1e-06


def halo_kernel(n_lat, n_lon, *refs):
    sources, landings, (send_sem, recv_sem) = refs[:8], refs[8:16], refs[16:]
    lat, lon = lax.axis_index("lat"), lax.axis_index("lon")
    steps = ((-1, 0), (1, 0), (0, -1), (0, 1), (-1, -1), (-1, 1), (1, -1), (1, 1))
    targets = [
        (lax.rem(lat + dy + n_lat, n_lat), lax.rem(lon + dx + n_lon, n_lon)) for dy, dx in steps
    ]
    barrier = pltpu.get_barrier_semaphore()
    for target in targets:
        pl.semaphore_signal(barrier, inc=1, device_id=target, device_id_type=MESH)
    pl.semaphore_wait(barrier, len(targets))
    copies = []
    for index, target in enumerate(targets):
        copy = pltpu.make_async_remote_copy(
            src_ref=sources[index], dst_ref=landings[index], send_sem=send_sem.at[index],
            recv_sem=recv_sem.at[index], device_id=target, device_id_type=MESH,
        )
        copy.start()
        copies.append(copy)
    for copy in copies:
        copy.wait()


def widened(fields):
    both = jnp.stack(fields)
    top, bottom = both[:, :, 0], both[:, :, -1]
    pieces = (
        top, bottom, both[:, :, :, 0], both[:, :, :, -1],
        top[:, :, 0], top[:, :, -1], bottom[:, :, 0], bottom[:, :, -1],
    )
    landed = pl.pallas_call(
        functools.partial(halo_kernel, lax.axis_size("lat"), lax.axis_size("lon")),
        out_shape=tuple(jax.ShapeDtypeStruct(p.shape, p.dtype) for p in pieces),
        in_specs=[pl.BlockSpec(memory_space=pltpu.VMEM)] * 8,
        out_specs=(pl.BlockSpec(memory_space=pltpu.VMEM),) * 8,
        scratch_shapes=[pltpu.SemaphoreType.DMA((8,)), pltpu.SemaphoreType.DMA((8,))],
        compiler_params=pltpu.CompilerParams(
            collective_id=1, has_side_effects=True, vmem_limit_bytes=24 * 1024 * 1024
        ),
        name="halo",
    )(*pieces)
    below, above, east, west, below_east, below_west, above_east, above_west = landed

    def row(start, middle, end):
        return jnp.concatenate([start[:, None, None], middle[:, None], end[:, None, None]], axis=2)

    wide = []
    for index, field in enumerate(fields):
        middle = jnp.concatenate(
            [west[index][:, :, None], field, east[index][:, :, None]], axis=2
        )
        first = row(above_west[index], above[index], above_east[index])
        last = row(below_west[index], below[index], below_east[index])
        wide.append(mask_poles(jnp.concatenate([first, middle, last], axis=1)))
    return wide


def mask_poles(wide_field):
    lat_index = lax.axis_index("lat")
    lat_count = lax.axis_size("lat")
    total_rows = wide_field.shape[1]
    row_ids = lax.broadcasted_iota(jnp.int32, (1, total_rows, 1, 1), 1)
    upper = jnp.logical_and(row_ids == 0, lat_index == 0)
    lower = jnp.logical_and(row_ids == total_rows - 1, lat_index == lat_count - 1)
    return jnp.where(jnp.logical_or(upper, lower), jnp.zeros((), wide_field.dtype), wide_field)


def input_taps(act_wide, grad_flat, lat_rows, lon_cols):

    def input_compute(first_row, row_count):
        tap_parts = []
        for tap_index in range(9):
            row_off, col_off = divmod(tap_index, 3)
            tap_slab = act_wide[
                :, row_off : row_off + lat_rows, col_off : col_off + lon_cols, :
            ].reshape(-1, row_count)
            tap_parts.append(
                lax.dot_general(
                    tap_slab,
                    grad_flat,
                    (((0,), (0,)), ((), ())),
                    preferred_element_type=jnp.float32,
                )
            )
        return jnp.stack(tap_parts, axis=1)

    return input_compute


def reduce_update_gather(
    n_lat, n_q, max_norm, part, master, one, two,
    gathered, new_master, new_one, new_two, clipped,
    core_in, sums, right_in, left_in, lat_out, lat_in, norm_out, norm_in,
    send_sem, recv_sem,
):
    lat = lax.axis_index("lat")
    lon = lax.axis_index("lon")
    core = lax.rem(lon, 2)
    q = lon // 2
    hops = n_q // 2
    half = n_lat // 2
    counter = [0]
    pending = []

    def at(lat_id, q_id, core_id):
        return (lat_id, q_id * 2 + core_id)

    partner = at(lat, q, 1 - core)
    right_q = lax.rem(q + 1, n_q)
    left_q = lax.rem(q + n_q - 1, n_q)
    right, left = at(lat, right_q, core), at(lat, left_q, core)
    q_peers = [at(lat, lax.rem(q + d, n_q), core) for d in range(1, n_q)]
    lat_peers = [at(lax.rem(lat + d, n_lat), q, core) for d in range(1, n_lat)]

    def send(src, dst, target):
        index = counter[0]
        counter[0] += 1
        copy = pltpu.make_async_remote_copy(
            src_ref=src, dst_ref=dst, send_sem=send_sem.at[index],
            recv_sem=recv_sem.at[index], device_id=target, device_id_type=MESH,
        )
        copy.start()
        pending.append(copy)
        return copy

    def wrap(index, size):
        return lax.rem(index + size, size)

    barrier = pltpu.get_barrier_semaphore()
    greeted = [partner] + q_peers + lat_peers
    for device in greeted:
        pl.semaphore_signal(barrier, inc=1, device_id=device, device_id_type=MESH)
    pl.semaphore_wait(barrier, len(greeted))

    order = []
    for step in range(hops):
        for block in (hops - step, -hops + step):
            if block % n_q not in order:
                order.append(block % n_q)
    order.append(0)
    core_copies = []
    for offset in order:
        block = lax.rem(q + offset, n_q)
        core_copies.append(
            send(part.at[:, :, block, 1 - core], core_in.at[:, :, block], partner)
        )
    arrived = {}

    def core_sum(offset):
        if offset in arrived:
            return
        arrived[offset] = True
        core_copies[order.index(offset)].wait_recv()
        block = lax.rem(q + offset, n_q)

        @pl.loop(0, n_lat)
        def _(row):
            sums[block, row] = (
                part[:, row, block, core] + core_in[:, row, block]
            ).astype(jnp.bfloat16)

    def add_into(block, low, high, source):
        @pl.loop(low, high)
        def _(row):
            sums[block, row] = (
                sums[block, row].astype(jnp.float32) + source[row].astype(jnp.float32)
            ).astype(jnp.bfloat16)

    ring = []
    for step in range(hops):
        right_off = (hops - step) % n_q
        left_off = (step - hops) % n_q
        core_sum(right_off)
        core_sum(left_off)
        right_block = lax.rem(q + right_off, n_q)
        left_block = lax.rem(q + left_off, n_q)
        if step == 0:
            ring.append((
                send(sums.at[right_block, pl.ds(0, half)], right_in.at[0, pl.ds(0, half)], right),
                send(sums.at[left_block, pl.ds(half, n_lat - half)],
                     left_in.at[0, pl.ds(half, n_lat - half)], left),
            ))
        else:
            from_left, from_right = ring[-1]
            bounds = (0, half, half, n_lat) if step == 1 else (0, n_lat, 0, n_lat)
            from_left.wait_recv()
            add_into(right_block, bounds[0], bounds[1], right_in.at[step - 1])
            going_right = send(sums.at[right_block], right_in.at[step], right)
            from_right.wait_recv()
            add_into(left_block, bounds[2], bounds[3], left_in.at[step - 1])
            ring.append((going_right, send(sums.at[left_block], left_in.at[step], left)))
    core_sum(0)
    for copy in ring[-1]:
        copy.wait_recv()

    def q_total(row):
        total = part[:, row, q, core] + core_in[:, row, q]
        if hops > 1:
            return (
                total + right_in[hops - 1, row].astype(jnp.float32)
                + left_in[hops - 1, row].astype(jnp.float32)
            )
        return total + jnp.where(
            row < half, right_in[0, row].astype(jnp.float32), left_in[0, row].astype(jnp.float32)
        )

    lat_copies = []
    for step in range(1, n_lat):
        target = lax.rem(lat + step, n_lat)
        lat_out[step - 1] = q_total(target).astype(jnp.bfloat16)
        lat_copies.append(send(lat_out.at[step - 1], lat_in.at[step - 1], lat_peers[step - 1]))
    grad = q_total(lat)
    for step, copy in enumerate(lat_copies):
        copy.wait_recv()
        grad = grad + lat_in[step].astype(jnp.float32)
    clipped[...] = grad

    square = jnp.sum(grad * grad)
    slot = 0
    for stage, peers in enumerate(([partner], q_peers, lat_peers)):
        norm_out[stage] = jnp.full(norm_out.shape[1:], square, jnp.float32)
        copies = []
        for target in peers:
            copies.append(send(norm_out.at[stage], norm_in.at[slot], target))
            slot += 1
        tile = norm_out[stage]
        for index, copy in enumerate(copies):
            copy.wait_recv()
            tile = tile + norm_in[slot - len(peers) + index]
        square = jnp.max(tile)
    square = jnp.full((1, 1), square, jnp.float32)
    clip_factor = jnp.minimum(1.0, max_norm / (jnp.sqrt(square) + norm_eps))

    @pl.loop(0, clipped.shape[0])
    def _(tap):
        scaled = clip_factor * clipped[tap]
        clipped[tap] = scaled
        first = beta_one * one[tap] + (1.0 - beta_one) * scaled
        second = beta_two * two[tap] + (1.0 - beta_two) * scaled * scaled
        new_one[tap] = first
        new_two[tap] = second
        first_hat = first / (1.0 - beta_one**step_count)
        second_hat = second / (1.0 - beta_two**step_count)
        updated = master[tap] - learn_rate * (
            first_hat / (jnp.sqrt(second_hat) + adam_eps) + decay_rate * master[tap]
        )
        new_master[tap] = updated
        gathered[core, q, lat, tap] = updated.astype(jnp.bfloat16)

    copies = [
        send(gathered.at[core, q, lat], gathered.at[core, q, lat], peer) for peer in lat_peers
    ]
    for copy in copies:
        copy.wait_recv()
    core_in_copies = []

    def to_partner(block, low, count):
        piece = gathered.at[core, block, pl.ds(low, count)]
        core_in_copies.append(send(piece, piece, partner))

    from_left = from_right = None
    for step in range(hops):
        last = step == hops - 1
        right_block = wrap(q - step, n_q)
        left_block = lax.rem(q + step, n_q)
        if from_left is not None:
            from_left.wait_recv()
        piece = gathered.at[core, right_block, pl.ds(0, half if last else n_lat)]
        going_right = send(piece, piece, right)
        if from_right is not None:
            from_right.wait_recv()
        low = half if last else 0
        piece = gathered.at[core, left_block, pl.ds(low, n_lat - low)]
        going_left = send(piece, piece, left)
        to_partner(right_block, 0, n_lat)
        if step > 0:
            to_partner(left_block, 0, n_lat)
        from_left, from_right = going_right, going_left
    far = lax.rem(q + hops, n_q)
    from_left.wait_recv()
    to_partner(far, 0, half)
    from_right.wait_recv()
    to_partner(far, half, n_lat - half)
    for copy in core_in_copies:
        copy.wait_recv()
    for copy in pending:
        copy.wait_send()


def fused_update(partial, master, one, two):
    n_lat, n_q = lax.axis_size("lat"), lax.axis_size("lon") // 2
    taps, rows, width = master.shape
    part = partial.reshape(taps, n_lat, n_q, 2, rows, width)
    max_norm = math.sqrt(float(partial.size))
    shard = jax.ShapeDtypeStruct(master.shape, jnp.float32)
    hops = n_q // 2
    half_type = jnp.bfloat16
    block = (n_lat, taps, rows, width)
    peers = n_q + n_lat - 1
    vmem = pl.BlockSpec(memory_space=pltpu.VMEM)
    copies = 64 + 8 * (n_q + n_lat)
    return pl.pallas_call(
        functools.partial(reduce_update_gather, n_lat, n_q, max_norm),
        out_shape=(
            jax.ShapeDtypeStruct((2, n_q) + block, half_type), shard, shard, shard, shard,
        ),
        in_specs=[vmem] * 4,
        out_specs=(vmem,) * 5,
        scratch_shapes=[
            pltpu.VMEM((taps, n_lat, n_q, rows, width), jnp.float32),
            pltpu.VMEM((n_q,) + block, half_type),
            pltpu.VMEM((hops,) + block, half_type),
            pltpu.VMEM((hops,) + block, half_type),
            pltpu.VMEM((n_lat - 1, taps, rows, width), half_type),
            pltpu.VMEM((n_lat - 1, taps, rows, width), half_type),
            pltpu.VMEM((3, 8, 128), jnp.float32),
            pltpu.VMEM((peers, 8, 128), jnp.float32),
            pltpu.SemaphoreType.DMA((copies,)),
            pltpu.SemaphoreType.DMA((copies,)),
        ],
        compiler_params=pltpu.CompilerParams(
            collective_id=0, has_side_effects=True, vmem_limit_bytes=60 * 1024 * 1024
        ),
        name="reduce_update_gather",
    )(part, master, one, two)


def per_device(activations, upstream, master, moment_one, moment_two):
    lat_rows = activations.shape[1]
    lon_cols = activations.shape[2]
    grad_flat = upstream.reshape(-1, upstream.shape[3])
    old_weights = master[:, ::-1].astype(jnp.bfloat16)
    old_full = lax.all_gather(old_weights, ("lat", "lon"), axis=0, tiled=True)
    act_wide, grad_wide = widened((activations, upstream))
    term_maker = input_taps(act_wide, grad_flat, lat_rows, lon_cols)
    partial = term_maker(jnp.int32(0), activations.shape[3])

    def by_tap(array):
        return jnp.transpose(array, (1, 0, 2))

    gathered, new_master, new_one, new_two, clipped = fused_update(
        by_tap(partial), by_tap(master), by_tap(moment_one), by_tap(moment_two)
    )
    new_weights = jnp.transpose(gathered, (2, 1, 0, 4, 3, 5)).reshape(
        activations.shape[3], gathered.shape[3], gathered.shape[5]
    )
    old_full, new_one = lax.optimization_barrier((old_full, new_one))
    input_grad = lax.conv_general_dilated(
        grad_wide,
        old_full.reshape(old_full.shape[0], 3, 3, old_full.shape[2]),
        (1, 1),
        "VALID",
        dimension_numbers=("NHWC", "OHWI", "NHWC"),
        preferred_element_type=jnp.float32,
    ).astype(jnp.bfloat16)
    return (
        input_grad, new_weights, by_tap(new_master), by_tap(new_one), by_tap(new_two),
        by_tap(clipped),
    )


def solution(mesh):
    in_specs = (
        P(None, "lat", "lon", None),
        P(None, "lat", "lon", None),
        P(("lat", "lon"), None, None),
        P(("lat", "lon"), None, None),
        P(("lat", "lon"), None, None),
    )
    out_specs = (
        P(None, "lat", "lon", None),
        P(),
        P(("lat", "lon"), None, None),
        P(("lat", "lon"), None, None),
        P(("lat", "lon"), None, None),
        P(("lat", "lon"), None, None),
    )
    return jax.shard_map(
        per_device, mesh=mesh, in_specs=in_specs, out_specs=out_specs, check_vma=False
    )
```

profile of v0, /device:TPU:0, one launch (start us, length us, event | category | flops | bytes accessed | tf_op | source)
XLA Modules:
  0.0 241.1 jit_solution(4245115340084497875)
XLA Ops:
  7.2 1.7 rev.5
  9.0 2.2 copy.118
  12.4 1.5 copy.65
  13.9 1.0 fusion.82
  15.4 46.0 %halo.1 = (bf16[2,4,90,512]{3,2,1,0:T(8,128)(2,1)S(1)}, bf16[2,4,90,512]{3,2,1,0:T(8,128)(2,1)S(1)}, bf16[2,4,4,512]{3,2,1,0:T(4,128)(2,1)S(1)}, bf16[2,4,4,512]...) custom-call(bf16[2,4,90,512]{3,2,1,0:T(8,128)(2,1)S(1)} %copy.47.ref, ...), custom_call_target="tpu_custom_call" | custom-call | tf_op jit(solution)/shard_map/halo/pallas_call | solution.py:57
  63.4 4.6 %fusion.5 = (bf16[6,4,92,512]{3,2,0,1:T(8,128)(2,1)S(1)}, bf16[4,6,92,512]{3,2,1,0:T(8,128)(2,1)S(1)}) fusion(bf16[4,1,92,512]{3,2,1,0:T(8,128)(2,1)S(1)} %maximum_bitcast_fusion.1, bf16[4,4,1,512]{3,2,1,0:T(2,128)(2,1)S(1)} %copy.55, bf16[4,4,90,512]{3,2,1,0:T(8,128)(2,1)S(1)} %copy.54, bf16[4,4,1,512]{3,2,1,0:T(2,128)(2,1)S(1)} %copy.53, ...), kind=kLoop, calls=%fused_computation.14 | loop fusion | flops 24870912 | bytes 9043974 | tf_op jit(solution)/shard_map/jit(_where)/select_n | solution.py:91
  67.9 1.7 copy.91
  69.7 0.9 pad.clone
  70.6 0.9 slice.144
  71.4 2.0 fusion.29
  73.5 2.0 fusion.35
  75.5 2.0 fusion.41
  77.5 2.0 fusion.47
  79.4 2.0 fusion.53
  81.5 2.0 fusion.59
  83.5 2.0 fusion.65
  85.5 2.1 fusion.71
  87.6 2.1 fusion.77
  89.7 120.2 %reduce_update_gather.1 = (bf16[2,4,4,9,16,512]{5,4,3,2,1,0:T(8,128)(2,1)}, f32[9,16,512]{2,1,0:T(8,128)}, f32[9,16,512]{2,1,0:T(8,128)}, f32[9,16,512]{2,1,0:T(8,128)}, f32[9,16,512]{2,1,0:T(8,128)}) custom-call(f32[9,4,4,2,16,512]{5,4,3,2,1,0:T(8,128)} %bitcast.61.part, f32[9,16,512]{2,1,0:T(8,128)} %bitcast.168, f32[9,16,512]{2,1,0:T(8,128)} %bitcast.169, ...), custom_call_target="tpu_custom_call" | custom-call | tf_op jit(solution)/shard_map/reduce_update_gather/pallas_call | solution.py:328
  210.0 5.3 %copy.81 = bf16[4,4,2,16,9,512]{5,3,2,1,0,4:T(8,128)(2,1)} copy(bf16[4,4,2,16,9,512]{5,3,4,0,1,2:T(8,128)(2,1)} %bitcast.167) | data formatting | bytes 9437184 | tf_op jit(solution)/shard_map/transpose | solution.py:370
  215.3 2.7 %fusion.1 = bf16[6,4,8,14,512]{4,1,3,2,0:T(4,128)(2,1)} fusion(bf16[6,4,7,2,512]{4,1,3,2,0:T(4,128)(2,1)S(1)} %copy-done.4, bf16[6,4,8,12,512]{4,1,3,2,0:T(4,128)(2,1)S(1)} %bitcast.164), kind=kLoop, calls=%fused_computation.9 | loop fusion | flops 8257536 | bytes 5455872 | tf_op jit(solution)/shard_map/conv_general_dilated | solution.py:374
  218.0 10.5 %select_convert_fusion = bf16[4,32,12,512]{3,1,2,0:T(8,128)(2,1)S(1)} fusion(pred[32,12]{0,1:T(8,128)(4,1)S(1)} %copy-done.9, bf16[512,3,3,512]{3,0,2,1:T(8,128)(2,1)} %bitcast.175, bf16[6,4,8,14,512]{4,1,3,2,0:T(4,128)(2,1)} %fusion.1), kind=kOutput, calls=%fused_computation.2 | convolution fusion | flops 7249330176 | bytes 9044352 | tf_op jit(solution)/shard_map/conv_general_dilated | solution.py:374
  228.5 1.2 copy.80
  229.8 1.6 slice_bitcast_fusion
  (60 shorter events, 6.3 us)
Async XLA Ops:
  7.2 4.1 %copy-start.2 = (bf16[4,4,90,512]{3,1,2,0:T(4,128)(2,1)S(1)}, bf16[4,4,90,512]{3,1,2,0:T(4,128)(2,1)}, u32[]{:S(2)}) copy-start(bf16[4,4,90,512]{3,1,2,0:T(4,128)(2,1)} %param.6) | copy-start | bytes 4423684
  7.2 210.8 %all-gather.2.cloned.1.call-start = ((), (), s32[]{:S(2)}) async-start(), calls=%async_computation | async-start | bytes 4866048 | tf_op jit(solution)/shard_map/all_gather | solution.py:359
  9.0 2.6 %copy-start.1 = (bf16[4,4,90,512]{3,1,2,0:T(4,128)(2,1)S(1)}, bf16[4,4,90,512]{3,1,2,0:T(4,128)(2,1)}, u32[]{:S(2)}) copy-start(bf16[4,4,90,512]{3,1,2,0:T(4,128)(2,1)} %param.5) | copy-start | bytes 4423684
  61.9 1.4 copy-start
  69.7 1.8 copy-start.3
  209.9 5.3 %copy-start.4 = (bf16[6,4,7,2,512]{4,1,3,2,0:T(4,128)(2,1)S(1)}, bf16[6,4,7,2,512]{4,1,3,2,0:T(4,128)(2,1)}, u32[]{:S(2)}) copy-start(bf16[6,4,7,2,512]{4,1,3,2,0:T(4,128)(2,1)} %slice.144) | copy-start | bytes 1032196
  215.3 2.7 %copy-start.9 = (pred[32,12]{0,1:T(8,128)(4,1)S(1)}, pred[32,12]{0,1:T(8,128)(4,1)}, u32[]{:S(2)}) copy-start(pred[32,12]{0,1:T(8,128)(4,1)} %constant.23) | copy-start | bytes 1156
  228.5 2.9 %copy-start.8 = (f32[9,16,512]{2,1,0:T(8,128)S(1)}, f32[9,16,512]{2,1,0:T(8,128)}, u32[]{:S(2)}) copy-start(f32[9,16,512]{2,1,0:T(8,128)} %get-tuple-element.32) | copy-start | bytes 884740
  229.8 2.4 copy-start.7
  229.8 3.1 %copy-start.6 = (f32[9,16,512]{2,1,0:T(8,128)S(1)}, f32[9,16,512]{2,1,0:T(8,128)}, u32[]{:S(2)}) copy-start(f32[9,16,512]{2,1,0:T(8,128)} %get-tuple-element.34) | copy-start | bytes 884740
  229.8 3.8 %copy-start.5 = (f32[9,16,512]{2,1,0:T(8,128)S(1)}, f32[9,16,512]{2,1,0:T(8,128)}, u32[]{:S(2)}) copy-start(f32[9,16,512]{2,1,0:T(8,128)} %get-tuple-element.35) | copy-start | bytes 884740
Sparse Core Ops, SparseCore 0:
  11.6 70.1 all-gather.1
where the time goes:
time: 241 us
  Pallas kernels  166 us (69%)
  matrix products  28.8 us (12%)
  local copies, waits for them, and re-layouts  22.8 us (9%)
  between operations  14.4 us (6%)
  other arithmetic  8.73 us (4%)
    pallas_call x1, Pallas kernels, fused_update(): pl.pallas_call(functools.partial(reduce_update_gather, n_lat, n_q, max_no...  120 us
    pallas_call x1, Pallas kernels, widened(): pl.pallas_call(functools.partial(halo_kernel, lax.axis_size('lat'), lax.a...  46 us
    dot_general x9, matrix products, input_compute(): lax.dot_general(tap_slab, grad_flat, (((0,), (0,)), ((), ())), preferred_...  18.3 us
    conv_general_dilated x1, matrix products, per_device(): lax.conv_general_dilated(grad_wide, old_full.reshape(old_full.shape[0], 3...  10.5 us
    unnamed x29, local copies, waits for them, and re-layouts  10.3 us
    transpose x1, local copies, waits for them, and re-layouts, per_device(): jnp.transpose(gathered, (2, 1, 0, 4, 3, 5))  5.32 us
  transfers between devices with their start and end apart: 1, of which 0 were waited for; matrix products, arithmetic and copies ran while one was open for 17% of the time, Pallas kernels for 69%

commit v1 on v0

--- a/solution.py
+++ b/solution.py
@@ -351,7 +351,535 @@
     )(part, master, one, two)
 
 
+LANE_TILE = 128
+ROW_TILE = 16
+
+
+def selector(shape, rows_of):
+    rows = lax.broadcasted_iota(jnp.int32, shape, 0)
+    cols = lax.broadcasted_iota(jnp.int32, shape, 1)
+    return jnp.where(rows_of(rows, cols), 1.0, 0.0).astype(jnp.bfloat16)
+
+
+def whole_step(
+    n_lat, n_q, max_norm, batch, lat_rows,
+    up, act, master, one, two,
+    input_grad, w_new, new_master, new_one, new_two, clipped,
+    fields, halo_out, halo_in, w_old, part, core_in, mine,
+    first_x, first_y, first_x_in, first_y_in, keep_x, keep_y,
+    second_x, second_y, second_x_in, second_y_in, last_out, last_in,
+    norm_out, norm_in, send_sem, recv_sem,
+):
+    lat = lax.axis_index("lat")
+    lon = lax.axis_index("lon")
+    n_lon = n_q * 2
+    core = lax.rem(lon, 2)
+    q = lon // 2
+    taps, rows, width = master.shape
+    cols = up.shape[0]
+    group_rows = batch * lat_rows
+    chunks, halo_rows = halo_out.shape[1], halo_out.shape[2]
+    chunk = cols // chunks
+    half = width // 2
+    counter = [0]
+    pending = []
+
+    def at(lat_id, q_id, core_id):
+        return (lat_id, q_id * 2 + core_id)
+
+    x_lat = lat + 1 - 2 * lax.rem(lat, 2)
+    y_lat = lax.rem(lat + 2, 4)
+    d_lat = x_lat + y_lat - lat
+    partner = at(lat, q, 1 - core)
+    x_peer, y_peer, d_peer = at(x_lat, q, core), at(y_lat, q, core), at(d_lat, q, core)
+
+    def across(k):
+        flipped = q
+        bit = 1
+        while bit < n_q:
+            if k & bit:
+                flipped = flipped + bit - 2 * bit * lax.rem(flipped // bit, 2)
+            bit *= 2
+        return flipped
+
+    z_ids = [across(k) for k in range(n_q)]
+    z_peers = [at(lat, z_ids[k], core) for k in range(1, n_q)]
+    west = (lat, lax.rem(lon + n_lon - 1, n_lon))
+    east = (lat, lax.rem(lon + 1, n_lon))
+    above = (jnp.maximum(lat - 1, 0), lon)
+    below = (jnp.minimum(lat + 1, n_lat - 1), lon)
+
+    def slots(count):
+        start = counter[0]
+        counter[0] += count
+        return start
+
+    def remote(src, dst, target, index):
+        return pltpu.make_async_remote_copy(
+            src_ref=src, dst_ref=dst, send_sem=send_sem.at[index],
+            recv_sem=recv_sem.at[index], device_id=target, device_id_type=MESH,
+        )
+
+    def send(src, dst, target):
+        copy = remote(src, dst, target, slots(1))
+        copy.start()
+        pending.append(copy)
+        return copy
+
+    barrier = pltpu.get_barrier_semaphore()
+    other_west = lax.rem(q + n_q - 1, n_q) * 2 + 1
+    other_east = lax.rem(q + 1, n_q) * 2
+    outside = (lat, jnp.where(core == 0, other_west, other_east))
+    greeted = [partner, outside, x_peer, y_peer, d_peer] + z_peers
+    for device in greeted:
+        pl.semaphore_signal(barrier, inc=1, device_id=device, device_id_type=MESH)
+
+    for tap in range(taps):
+        w_old[tap, lat, q, core] = master[tap].astype(jnp.bfloat16)
+
+    @pl.loop(0, cols)
+    def _(j):
+        fields[1, j + 1] = up[j]
+
+    def last_row(index):
+        return lax.rem(index, lat_rows) == lat_rows - 1
+
+    def first_row(index):
+        return lax.rem(index, lat_rows) == 0
+
+    span = chunk * group_rows
+    picked = chunk * batch
+    take = [
+        selector((halo_rows, span), lambda m, n: n == m * lat_rows),
+        selector((halo_rows, span), lambda m, n: n == m * lat_rows + lat_rows - 1),
+    ]
+
+    @pl.loop(0, chunks)
+    def _(c):
+        block = up[pl.ds(c * chunk, chunk)].reshape(span, width)
+        for side in range(2):
+            halo_out[side, c] = jnp.dot(
+                take[side], block, preferred_element_type=jnp.float32
+            ).astype(jnp.bfloat16)
+
+    pl.semaphore_wait(barrier, len(greeted))
+
+    class Gather:
+        def __init__(self, buffer, cut):
+            self.buffer, self.cut = buffer, cut
+            self.to_z, self.to_x, self.to_y, self.to_core = {}, {}, {}, []
+            self.diag_x, self.diag_y = {}, {}
+
+        def block(self, lat_id, q_id, low, high):
+            return self.buffer.at[:, lat_id, q_id, core, :, pl.ds(low, high - low)]
+
+        def give(self, lat_id, q_id, low, high, target):
+            piece = self.block(lat_id, q_id, low, high)
+            return send(piece, piece, target)
+
+        def spread(self, k):
+            self.to_x[k] = self.give(lat, z_ids[k], 0, width, x_peer)
+            self.to_y[k] = self.give(lat, z_ids[k], 0, width, y_peer)
+            self.to_core.append(self.give(lat, z_ids[k], 0, width, partner))
+
+        def start_z(self):
+            for k in range(1, n_q):
+                self.to_z[k] = self.give(lat, q, 0, width, z_peers[k - 1])
+
+        def start(self):
+            self.start_z()
+            self.spread(0)
+
+        def from_z(self, k):
+            self.to_z[k].wait_recv()
+            self.spread(k)
+
+        def relay(self, k):
+            self.to_x[k].wait_recv()
+            self.diag_y[k] = self.give(x_lat, z_ids[k], 0, self.cut, y_peer)
+            self.to_core.append(self.give(x_lat, z_ids[k], 0, width, partner))
+            self.to_y[k].wait_recv()
+            if self.cut < width:
+                self.diag_x[k] = self.give(y_lat, z_ids[k], self.cut, width, x_peer)
+            self.to_core.append(self.give(y_lat, z_ids[k], 0, width, partner))
+
+        def close(self, k):
+            self.diag_y[k].wait_recv()
+            self.to_core.append(self.give(d_lat, z_ids[k], 0, self.cut, partner))
+            if self.cut < width:
+                self.diag_x[k].wait_recv()
+                self.to_core.append(self.give(d_lat, z_ids[k], self.cut, width, partner))
+
+        def finish(self):
+            for copy in self.to_core:
+                copy.wait_recv()
+
+    old = Gather(w_old, width)
+    old.start_z()
+
+    up_slot, down_slot = slots(1), slots(1)
+    to_above = remote(halo_out.at[0], halo_in.at[0], above, up_slot)
+    to_below = remote(halo_out.at[1], halo_in.at[1], below, down_slot)
+    has_above, has_below = lat > 0, lat < n_lat - 1
+
+    @pl.when(has_above)
+    def _():
+        to_above.start()
+
+    @pl.when(has_below)
+    def _():
+        to_below.start()
+
+    def edges(field):
+        to_west = send(fields.at[field, 1], fields.at[field, cols + 1], west)
+        to_east = send(fields.at[field, cols], fields.at[field, 0], east)
+        return to_west, to_east
+
+    middle_edges = edges(1)
+    old.spread(0)
+
+    acts = act[...].reshape(cols * group_rows, width)
+    part_slot = slots(taps)
+
+    def part_copy(tap):
+        return remote(
+            part.at[tap, :, :, 1 - core], core_in.at[tap], partner, part_slot + tap
+        )
+
+    def weight_taps(group):
+        @pl.loop(0, 3)
+        def _(s):
+            shifted = fields[group, pl.ds(2 - s, cols)].reshape(cols * group_rows, width)
+            tap = group * 3 + s
+            part[tap] = lax.dot_general(
+                acts, shifted, (((0,), (0,)), ((), ())), preferred_element_type=jnp.float32
+            ).reshape(n_lat, n_q, 2, rows, width)
+            part_copy(tap).start()
+
+    first, second, third = {}, {}, {}
+
+    def reduce_first(group):
+        @pl.loop(0, 3)
+        def _(s):
+            tap = group * 3 + s
+            part_copy(tap).wait_recv()
+            for k in range(n_q):
+                def total(lat_id):
+                    return part[tap, lat_id, k, core] + core_in[tap, lat_id, k]
+
+                mine[tap, k] = total(lat)
+                value = total(x_lat)
+                keep_x[tap, k] = value[:, :half]
+                first_x[tap, 0, k] = value[:, half:].astype(jnp.bfloat16)
+                value = total(y_lat)
+                first_y[tap, 0, k] = value[:, :half].astype(jnp.bfloat16)
+                keep_y[tap, k] = value[:, half:]
+                value = total(d_lat)
+                first_y[tap, 1, k] = value[:, :half].astype(jnp.bfloat16)
+                first_x[tap, 1, k] = value[:, half:].astype(jnp.bfloat16)
+
+        piece = pl.ds(group * 3, 3)
+        first[group] = (
+            send(first_x.at[piece], first_x_in.at[piece], x_peer),
+            send(first_y.at[piece], first_y_in.at[piece], y_peer),
+        )
+
+    def reduce_second(group):
+        piece = pl.ds(group * 3, 3)
+        for copy in first[group]:
+            copy.wait_recv()
+
+        @pl.loop(0, 3)
+        def _(s):
+            tap = group * 3 + s
+            for k in range(n_q):
+                second_x[tap, k] = (
+                    keep_x[tap, k] + first_y_in[tap, 1, k].astype(jnp.float32)
+                ).astype(jnp.bfloat16)
+                second_y[tap, k] = (
+                    keep_y[tap, k] + first_x_in[tap, 1, k].astype(jnp.float32)
+                ).astype(jnp.bfloat16)
+
+        second[group] = (
+            send(second_x.at[piece], second_x_in.at[piece], x_peer),
+            send(second_y.at[piece], second_y_in.at[piece], y_peer),
+        )
+
+    def reduce_third(group):
+        piece = pl.ds(group * 3, 3)
+        for copy in second[group]:
+            copy.wait_recv()
+
+        @pl.loop(0, 3)
+        def _(s):
+            tap = group * 3 + s
+            for k in range(n_q):
+                low = (
+                    mine[tap, k, :, :half] + first_y_in[tap, 0, k].astype(jnp.float32)
+                    + second_x_in[tap, k].astype(jnp.float32)
+                )
+                high = (
+                    mine[tap, k, :, half:] + first_x_in[tap, 0, k].astype(jnp.float32)
+                    + second_y_in[tap, k].astype(jnp.float32)
+                )
+                mine[tap, k, :, :half] = low
+                mine[tap, k, :, half:] = high
+            for k in range(1, n_q):
+                last_out[k - 1, tap] = mine[tap, z_ids[k]].astype(jnp.bfloat16)
+
+        third[group] = [
+            send(last_out.at[k - 1, piece], last_in.at[k - 1, piece], z_peers[k - 1])
+            for k in range(1, n_q)
+        ]
+
+    for copy in middle_edges:
+        copy.wait_recv()
+    weight_taps(1)
+    for k in range(1, n_q):
+        old.from_z(k)
+    reduce_first(1)
+
+    @pl.when(has_below)
+    def _():
+        to_above.wait_recv()
+
+    @pl.when(has_above)
+    def _():
+        to_below.wait_recv()
+
+    @pl.when(jnp.logical_not(has_below))
+    def _():
+        halo_in[0] = jnp.zeros(halo_in.shape[1:], halo_in.dtype)
+
+    @pl.when(jnp.logical_not(has_above))
+    def _():
+        halo_in[1] = jnp.zeros(halo_in.shape[1:], halo_in.dtype)
+
+    shift = [
+        selector((span, span), lambda m, n: jnp.logical_and(n == m + 1, jnp.logical_not(last_row(m)))),
+        selector((span, span), lambda m, n: jnp.logical_and(n == m - 1, jnp.logical_not(first_row(m)))),
+    ]
+    place = [
+        selector((span, halo_rows), lambda m, n: jnp.logical_and(n == m // lat_rows, last_row(m))),
+        selector((span, halo_rows), lambda m, n: jnp.logical_and(n == m // lat_rows, first_row(m))),
+    ]
+
+    @pl.loop(0, chunks)
+    def _(c):
+        block = up[pl.ds(c * chunk, chunk)].reshape(span, width)
+        for side in range(2):
+            moved = jnp.dot(shift[side], block, preferred_element_type=jnp.float32)
+            moved = moved + jnp.dot(
+                place[side], halo_in[side, c], preferred_element_type=jnp.float32
+            )
+            fields[2 * side, pl.ds(1 + c * chunk, chunk)] = moved.astype(jnp.bfloat16).reshape(
+                chunk, group_rows, width
+            )
+
+    upper_edges, lower_edges = edges(0), edges(2)
+    for copy in upper_edges:
+        copy.wait_recv()
+    weight_taps(0)
+    reduce_first(0)
+    for k in range(n_q):
+        old.relay(k)
+    reduce_second(1)
+    for copy in lower_edges:
+        copy.wait_recv()
+    weight_taps(2)
+    reduce_first(2)
+    reduce_second(0)
+    reduce_third(1)
+    for k in range(n_q):
+        old.close(k)
+    reduce_second(2)
+    reduce_third(0)
+    reduce_third(2)
+
+    for group in range(3):
+        for copy in third[group]:
+            copy.wait_recv()
+    grad_square = jnp.zeros((rows, width), jnp.float32)
+
+    def finish_tap(tap, total):
+        grad = mine[tap, q]
+        for k in range(n_q - 1):
+            grad = grad + last_in[k, tap].astype(jnp.float32)
+        clipped[tap] = grad
+        return total + grad * grad
+
+    grad_square = lax.fori_loop(0, taps, finish_tap, grad_square)
+    square = jnp.sum(grad_square)
+
+    old.finish()
+    piece_cols = cols // 2
+
+    def input_piece(index):
+        total = None
+        for tap in range(taps):
+            r, s = divmod(tap, 3)
+            shifted = fields[r, pl.ds(index * piece_cols + 2 - s, piece_cols)]
+            product = lax.dot_general(
+                shifted.reshape(piece_cols * group_rows, width),
+                w_old[tap].reshape(-1, width),
+                (((1,), (1,)), ((), ())), preferred_element_type=jnp.float32,
+            )
+            total = product if total is None else total + product
+        input_grad[pl.ds(index * piece_cols, piece_cols)] = total.astype(jnp.bfloat16).reshape(
+            piece_cols, group_rows, width
+        )
+
+    slot = 0
+    for stage, peers in enumerate(([partner], z_peers, [x_peer, y_peer, d_peer])):
+        norm_out[stage] = jnp.full(norm_out.shape[1:], square, jnp.float32)
+        copies = []
+        for index, target in enumerate(peers):
+            copies.append(send(norm_out.at[stage], norm_in.at[slot + index], target))
+        tile = norm_out[stage]
+        for index, copy in enumerate(copies):
+            copy.wait_recv()
+            tile = tile + norm_in[slot + index]
+        slot += len(peers)
+        square = jnp.max(tile)
+    square = jnp.full((1, 1), square, jnp.float32)
+    clip_factor = jnp.minimum(1.0, max_norm / (jnp.sqrt(square) + norm_eps))
+
+    @pl.loop(0, taps)
+    def _(tap):
+        scaled = clip_factor * clipped[tap]
+        clipped[tap] = scaled
+        moment = beta_one * one[tap] + (1.0 - beta_one) * scaled
+        spread = beta_two * two[tap] + (1.0 - beta_two) * scaled * scaled
+        new_one[tap] = moment
+        new_two[tap] = spread
+        first_hat = moment / (1.0 - beta_one**step_count)
+        second_hat = spread / (1.0 - beta_two**step_count)
+        updated = master[tap] - learn_rate * (
+            first_hat / (jnp.sqrt(second_hat) + adam_eps) + decay_rate * master[tap]
+        )
+        new_master[tap] = updated
+        w_new[tap, lat, q, core] = updated.astype(jnp.bfloat16)
+
+    new = Gather(w_new, half)
+    new.start()
+    input_piece(0)
+    for k in range(1, n_q):
+        new.from_z(k)
+    for k in range(n_q):
+        new.relay(k)
+    input_piece(1)
+    for k in range(n_q):
+        new.close(k)
+    new.finish()
+
+    @pl.when(has_above)
+    def _():
+        to_above.wait_send()
+
+    @pl.when(has_below)
+    def _():
+        to_below.wait_send()
+
+    @pl.loop(0, taps)
+    def _(tap):
+        part_copy(tap).wait_send()
+
+    for copy in pending:
+        copy.wait_send()
+
+
+def fused_step(up, act, master, one, two, batch, lat_rows):
+    n_lat, n_q = lax.axis_size("lat"), lax.axis_size("lon") // 2
+    taps, rows, width = master.shape
+    cols, group_rows, _ = up.shape
+    half = width // 2
+    chunk = max(c for c in range(1, 17) if cols % c == 0)
+    chunks = cols // chunk
+    halo_rows = -(-chunk * batch // ROW_TILE) * ROW_TILE
+    max_norm = math.sqrt(float(n_lat * n_q * 2 * taps * rows * width))
+    bf16, f32 = jnp.bfloat16, jnp.float32
+    shard = jax.ShapeDtypeStruct(master.shape, f32)
+    whole = (taps, n_lat, n_q, 2, rows, width)
+    side = (taps, n_q, rows, half)
+    vmem = pl.BlockSpec(memory_space=pltpu.VMEM)
+    peers = n_q + n_lat - 1
+    copies = 128 + 16 * (n_q + n_lat)
+    return pl.pallas_call(
+        functools.partial(whole_step, n_lat, n_q, max_norm, batch, lat_rows),
+        out_shape=(
+            jax.ShapeDtypeStruct(up.shape, bf16), jax.ShapeDtypeStruct(whole, bf16),
+            shard, shard, shard, shard,
+        ),
+        in_specs=[vmem] * 5,
+        out_specs=(vmem,) * 6,
+        scratch_shapes=[
+            pltpu.VMEM((3, cols + 2, group_rows, width), bf16),
+            pltpu.VMEM((2, chunks, halo_rows, width), bf16),
+            pltpu.VMEM((2, chunks, halo_rows, width), bf16),
+            pltpu.VMEM(whole, bf16),
+            pltpu.VMEM(whole, f32),
+            pltpu.VMEM((taps, n_lat, n_q, rows, width), f32),
+            pltpu.VMEM((taps, n_q, rows, width), f32),
+            pltpu.VMEM((taps, 2) + side[1:], bf16),
+            pltpu.VMEM((taps, 2) + side[1:], bf16),
+            pltpu.VMEM((taps, 2) + side[1:], bf16),
+            pltpu.VMEM((taps, 2) + side[1:], bf16),
+            pltpu.VMEM(side, f32),
+            pltpu.VMEM(side, f32),
+            pltpu.VMEM(side, bf16),
+            pltpu.VMEM(side, bf16),
+            pltpu.VMEM(side, bf16),
+            pltpu.VMEM(side, bf16),
+            pltpu.VMEM((n_q - 1, taps, rows, width), bf16),
+            pltpu.VMEM((n_q - 1, taps, rows, width), bf16),
+            pltpu.VMEM((3, 8, LANE_TILE), f32),
+            pltpu.VMEM((peers, 8, LANE_TILE), f32),
+            pltpu.SemaphoreType.DMA((copies,)),
+            pltpu.SemaphoreType.DMA((copies,)),
+        ],
+        compiler_params=pltpu.CompilerParams(
+            collective_id=2, has_side_effects=True, vmem_limit_bytes=62 * 1024 * 1024
+        ),
+        name="whole_step",
+    )(up, act, master, one, two)
+
+
+def takes_fused(activations, master):
+    n_lat, n_q = lax.axis_size("lat"), lax.axis_size("lon") // 2
+    batch, lat_rows, cols, _ = activations.shape
+    return (
+        n_lat == 4 and n_q & (n_q - 1) == 0 and n_q > 1 and master.shape[0] % ROW_TILE == 0
+        and (batch * lat_rows) % ROW_TILE == 0 and cols % 2 == 0
+        and master.shape[2] % (2 * LANE_TILE) == 0 and master.shape[1] == 9
+    )
+
+
 def per_device(activations, upstream, master, moment_one, moment_two):
+    if not takes_fused(activations, master):
+        return per_device_general(activations, upstream, master, moment_one, moment_two)
+    batch, lat_rows, cols, width = activations.shape
+
+    def by_col(field):
+        return jnp.transpose(field, (2, 0, 1, 3)).reshape(cols, batch * lat_rows, width)
+
+    def by_tap(array):
+        return jnp.transpose(array, (1, 0, 2))
+
+    input_grad, gathered, new_master, new_one, new_two, clipped = fused_step(
+        by_col(upstream), by_col(activations), by_tap(master), by_tap(moment_one),
+        by_tap(moment_two), batch, lat_rows,
+    )
+    input_grad = jnp.transpose(
+        input_grad.reshape(cols, batch, lat_rows, width), (1, 2, 0, 3)
+    )
+    new_weights = by_tap(gathered.reshape(gathered.shape[0], -1, gathered.shape[-1]))
+    return (
+        input_grad, new_weights, by_tap(new_master), by_tap(new_one), by_tap(new_two),
+        by_tap(clipped),
+    )
+
+
+def per_device_general(activations, upstream, master, moment_one, moment_two):
     lat_rows = activations.shape[1]
     lon_cols = activations.shape[2]
     grad_flat = upstream.reshape(-1, upstream.shape[3])

time: 241 us -> 135 us (0.56)
  Pallas kernels: 166 us -> 116 us
  matrix products: 28.8 us -> 0 us
  between operations: 14.4 us -> 0.68 us
  other arithmetic: 8.73 us -> 0 us
  local copies, waits for them, and re-layouts: 22.8 us -> 18.4 us
    pallas_call x2 -> x1, Pallas kernels: 166 us -> 116 us  [fused_step(): pl.pallas_call(functools.partial(whole_step, n_lat, n_q, max_norm, batch,...]
    dot_general x9 -> x0, matrix products: 18.3 us -> none  [input_compute(): lax.dot_general(tap_slab, grad_flat, (((0,), (0,)), ((), ())), preferred_...]
    conv_general_dilated x1 -> x0, matrix products: 10.5 us -> none  [per_device(): lax.conv_general_dilated(grad_wide, old_full.reshape(old_full.shape[0], 3...]
    reshape x0 -> x4, local copies, waits for them, and re-layouts: none -> 7.01 us  [the longest x2 4.42 us: per_device(): input_grad.reshape(cols, batch, lat_rows, width)]
    select_n x1 -> x0, other arithmetic: 4.55 us -> none  [mask_poles(): jnp.where(jnp.logical_or(upper, lower), jnp.zeros((), wide_field.dtype),...]
    convert_element_type x2 -> x0, local copies, waits for them, and re-layouts: 2.83 us -> none  [per_device(): input_grad = lax.conv_general_dilated(grad_wide, old_full.reshape(old_ful...]
    conv_general_dilated x1 -> x0, other arithmetic: 2.71 us -> none  [per_device(): lax.conv_general_dilated(grad_wide, old_full.reshape(old_full.shape[0], 3...]
    transpose x1 -> x2, local copies, waits for them, and re-layouts: 5.32 us -> 3.01 us  [by_col(): jnp.transpose(field, (2, 0, 1, 3)).reshape(cols, batch * lat_rows, width)]
  transfers between devices with their start and end apart: 1 -> 0, of which waited for: 0 -> 0; matrix products, arithmetic and copies ran while one was open for 17% -> 0% of each run, Pallas kernels for 69% -> 0%
where the time goes in v1:
time: 135 us
  Pallas kernels  116 us (86%)
  local copies, waits for them, and re-layouts  18.4 us (14%)
    pallas_call x1, Pallas kernels, fused_step(): pl.pallas_call(functools.partial(whole_step, n_lat, n_q, max_norm, batch,...  116 us
    unnamed x15, local copies, waits for them, and re-layouts  8.38 us
    reshape x2, local copies, waits for them, and re-layouts, per_device(): input_grad.reshape(cols, batch, lat_rows, width)  4.42 us
    transpose x2, local copies, waits for them, and re-layouts, by_col(): jnp.transpose(field, (2, 0, 1, 3)).reshape(cols, batch * lat_rows, width)  3.01 us

profile of v1, /device:TPU:0, one launch (start us, length us, event | category | flops | bytes accessed | tf_op | source)
XLA Modules:
  0.0 134.6 jit_solution(17787903328588907)
XLA Ops:
  0.6 2.2 %copy.12 = bf16[90,4,4,512]{3,2,1,0:T(4,128)(2,1)S(1)} copy(bf16[90,4,4,512]{3,2,0,1:T(4,128)(2,1)} %bitcast.16) | data formatting | bytes 2949120 | tf_op jit(solution)/shard_map/transpose | solution.py:863
  2.8 0.0 copy-start
  2.8 1.3 reshape.25.act
  4.1 0.6 copy-done
  4.7 0.8 copy.11
  5.6 1.3 reshape.24.up
  6.9 115.6 %whole_step.1 = (bf16[90,16,512]{2,1,0:T(8,128)(2,1)}, bf16[9,4,4,2,16,512]{5,4,3,2,1,0:T(8,128)(2,1)}, f32[9,16,512]{2,1,0:T(8,128)}, f32[9,16,512]{2,1,0:T(8,1...) custom-call(bf16[90,16,512]{2,1,0:T(8,128)(2,1)} %reshape.24.up, bf16[90,16,512]{2,1,0:T(8,128)(2,1)} %reshape.25.act, ...), custom_call_target="tpu_custom_call" | custom-call | tf_op jit(solution)/shard_map/whole_step/pallas_call | solution.py:807
  122.4 2.8 %reshape.26 = bf16[90,4,4,512]{3,2,1,0:T(4,128)(2,1)S(1)} reshape(bf16[90,16,512]{2,1,0:T(8,128)(2,1)} %get-tuple-element.12) | data formatting | bytes 2949120 | tf_op jit(solution)/shard_map/reshape | solution.py:873
  125.2 1.6 %copy.15 = bf16[90,4,4,512]{3,2,0,1:T(4,128)(2,1)} copy(bf16[90,4,4,512]{3,2,1,0:T(4,128)(2,1)S(1)} %reshape.26) | data formatting | bytes 2949120 | tf_op jit(solution)/shard_map/reshape | solution.py:873
  126.9 0.0 copy-start.4
  126.9 0.0 copy-start.3
  126.9 0.0 copy-start.2
  126.9 4.9 %copy.21 = bf16[512,9,512]{2,0,1:T(8,128)(2,1)} copy(bf16[512,9,512]{2,0,1:T(8,128)(2,1)} %bitcast.15) | data formatting | bytes 9437184
  131.8 0.0 copy-done.4
  131.8 0.0 copy-start.1
  131.8 0.7 copy.22
  132.5 0.0 copy-done.3
  132.5 0.7 copy.23
  133.2 0.0 copy-done.2
  133.2 0.7 copy.24
  133.9 0.0 copy-done.1
  133.9 0.7 copy.25
Async XLA Ops:
  2.8 1.9 %copy-start = (bf16[4,4,90,512]{3,1,2,0:T(4,128)(2,1)S(1)}, bf16[4,4,90,512]{3,1,2,0:T(4,128)(2,1)}, u32[]{:S(2)}) copy-start(bf16[4,4,90,512]{3,1,2,0:T(4,128)(2,1)} %param.6) | copy-start | bytes 4423684
  126.9 4.9 %copy-start.4 = (f32[9,16,512]{2,1,0:T(8,128)S(1)}, f32[9,16,512]{2,1,0:T(8,128)}, u32[]{:S(2)}) copy-start(f32[9,16,512]{2,1,0:T(8,128)} %get-tuple-element.14) | copy-start | bytes 884740
  126.9 5.6 %copy-start.3 = (f32[9,16,512]{2,1,0:T(8,128)S(1)}, f32[9,16,512]{2,1,0:T(8,128)}, u32[]{:S(2)}) copy-start(f32[9,16,512]{2,1,0:T(8,128)} %get-tuple-element.15) | copy-start | bytes 884740
  126.9 6.3 %copy-start.2 = (f32[9,16,512]{2,1,0:T(8,128)S(1)}, f32[9,16,512]{2,1,0:T(8,128)}, u32[]{:S(2)}) copy-start(f32[9,16,512]{2,1,0:T(8,128)} %get-tuple-element.16) | copy-start | bytes 884740
  131.8 2.2 %copy-start.1 = (f32[9,16,512]{2,1,0:T(8,128)S(1)}, f32[9,16,512]{2,1,0:T(8,128)}, u32[]{:S(2)}) copy-start(f32[9,16,512]{2,1,0:T(8,128)} %get-tuple-element.17) | copy-start | bytes 884740

commit v2 on v0

--- a/solution.py
+++ b/solution.py
@@ -351,7 +351,788 @@
     )(part, master, one, two)
 
 
+LANE_TILE = 128
+ROW_TILE = 16
+OLD_LINE_TAPS = 6
+NEW_LINE_TAPS = 2
+
+
+def selector(shape, rows_of):
+    rows = lax.broadcasted_iota(jnp.int32, shape, 0)
+    cols = lax.broadcasted_iota(jnp.int32, shape, 1)
+    return jnp.where(rows_of(rows, cols), 1.0, 0.0).astype(jnp.bfloat16)
+
+
+def whole_step(
+    n_lat, n_q, max_norm,
+    up_hbm, act_hbm, master_hbm, one_hbm, two_hbm,
+    input_grad, w_new, new_master, new_one, new_two, clipped,
+    master, one, two, up_raw, act_raw, acts, fields, halo_out, halo_in, halo_pass, w_old, part, core_in, mine, keep,
+    first, first_in, second, second_in, last_out, last_in,
+    norm_out, norm_in, load_sem, send_sem, recv_sem,
+):
+    lat = lax.axis_index("lat")
+    lon = lax.axis_index("lon")
+    n_lon = n_q * 2
+    core = lax.rem(lon, 2)
+    q = lon // 2
+    taps, rows, width = master.shape
+    cols, batch, lat_rows, _ = up_raw.shape
+    group_rows = batch * lat_rows
+    chunks, halo_rows = halo_out.shape[1], halo_out.shape[2]
+    chunk = cols // chunks
+    span = chunk * group_rows
+    half = width // 2
+    counter = [0]
+    pending, guarded = [], []
+
+    def at(lat_id, q_id, core_id):
+        return (lat_id, q_id * 2 + core_id)
+
+    x_lat = lat + 1 - 2 * lax.rem(lat, 2)
+    y_lat = lax.rem(lat + 2, 4)
+    d_lat = x_lat + y_lat - lat
+    partner = at(lat, q, 1 - core)
+    x_peer, y_peer, d_peer = at(x_lat, q, core), at(y_lat, q, core), at(d_lat, q, core)
+
+    def across(k):
+        flipped = q
+        bit = 1
+        while bit < n_q:
+            if k & bit:
+                flipped = flipped + bit - 2 * bit * lax.rem(flipped // bit, 2)
+            bit *= 2
+        return flipped
+
+    z_ids = [across(k) for k in range(n_q)]
+    z_peers = [at(lat, z_ids[k], core) for k in range(1, n_q)]
+    next_z, last_z = at(lat, jnp.minimum(q + 1, n_q - 1), core), at(lat, jnp.maximum(q - 1, 0), core)
+    z_twins = [at(lat, z_ids[k], 1 - core) for k in range(1, n_q)]
+    west = (lat, lax.rem(lon + n_lon - 1, n_lon))
+    east = (lat, lax.rem(lon + 1, n_lon))
+    above = (jnp.maximum(lat - 1, 0), lon)
+    below = (jnp.minimum(lat + 1, n_lat - 1), lon)
+
+    def slots(count):
+        start = counter[0]
+        counter[0] += count
+        return start
+
+    def remote(src, dst, target, index):
+        return pltpu.make_async_remote_copy(
+            src_ref=src, dst_ref=dst, send_sem=send_sem.at[index],
+            recv_sem=recv_sem.at[index], device_id=target, device_id_type=MESH,
+        )
+
+    def send(src, dst, target):
+        copy = remote(src, dst, target, slots(1))
+        copy.start()
+        pending.append(copy)
+        return copy
+
+    def send_if(condition, src, dst, target):
+        copy = remote(src, dst, target, slots(1))
+
+        @pl.when(condition)
+        def _():
+            copy.start()
+
+        guarded.append((condition, copy))
+        return copy
+
+    barrier = pltpu.get_barrier_semaphore()
+    greeted = [partner, x_peer, y_peer, d_peer] + z_peers + z_twins
+    for device in greeted:
+        pl.semaphore_signal(barrier, inc=1, device_id=device, device_id_type=MESH)
+
+    def load(source, target, base):
+        copies = [
+            pltpu.make_async_copy(source.at[b], target.at[:, b], load_sem.at[base + b])
+            for b in range(batch)
+        ]
+        for copy in copies:
+            copy.start()
+        return copies
+
+    def load_whole(source, target, index):
+        copy = pltpu.make_async_copy(source, target, load_sem.at[index])
+        copy.start()
+        return copy
+
+    master_load = load_whole(master_hbm, master, 2 * batch)
+    up_load, act_load = load(up_hbm, up_raw, 0), load(act_hbm, act_raw, batch)
+    one_load = load_whole(one_hbm, one, 2 * batch + 1)
+    two_load = load_whole(two_hbm, two, 2 * batch + 2)
+    master_load.wait()
+    for tap in range(taps):
+        w_old[tap, lat, q, core] = master[tap].astype(jnp.bfloat16)
+
+    class Gather:
+        def __init__(self, buffer, cut, line_taps):
+            self.buffer, self.cut = buffer, cut
+            self.line_taps = line_taps
+            self.line = pl.ds(0, line_taps)
+            self.rest = pl.ds(line_taps, taps - line_taps)
+            self.has_rest = line_taps < taps
+            self.line_x = self.line_y = self.line_d = None
+            self.going_up, self.going_down, self.line_core = {}, {}, []
+            self.to_z, self.to_x, self.to_y, self.to_core = {}, {}, {}, []
+            self.diag_x, self.diag_y = {}, {}
+
+        def give(self, lat_id, q_id, low, high, target):
+            piece = self.buffer.at[
+                self.rest, lat_id, q_id, core, :, pl.ds(low, high - low)
+            ]
+            return send(piece, piece, target)
+
+        def line_block(self, lat_id, q_id):
+            return self.buffer.at[self.line, lat_id, q_id, core]
+
+        def line_give(self, lat_id, target):
+            piece = self.line_block(lat_id, q)
+            return send(piece, piece, target)
+
+        def line_up(self, name, lat_id, step):
+            block = jnp.maximum(q - step, 0)
+            piece = self.line_block(lat_id, block)
+            here = q >= step
+            self.going_up[name, step + 1] = send_if(
+                jnp.logical_and(here, q < n_q - 1), piece, piece, next_z
+            )
+            if step:
+                self.line_core.append((here, send_if(here, piece, piece, partner)))
+
+        def line_down(self, name, lat_id, step):
+            block = jnp.minimum(q + step, n_q - 1)
+            piece = self.line_block(lat_id, block)
+            here = q < n_q - step
+            self.going_down[name, step + 1] = send_if(
+                jnp.logical_and(here, q > 0), piece, piece, last_z
+            )
+            if step:
+                self.line_core.append((here, send_if(here, piece, piece, partner)))
+
+        def line_begin(self, name, lat_id):
+            self.line_up(name, lat_id, 0)
+            self.line_down(name, lat_id, 0)
+            self.to_core.append(self.line_give(lat_id, partner))
+
+        def line_start(self):
+            if not self.line_taps:
+                return
+            self.line_x = self.line_give(lat, x_peer)
+            self.line_begin("own", lat)
+
+        def line_start_y(self):
+            if not self.line_taps:
+                return
+            self.line_y = self.line_give(lat, y_peer)
+
+        def line_cross(self):
+            if not self.line_taps:
+                return
+            self.line_x.wait_recv()
+            self.line_d = self.line_give(x_lat, y_peer)
+            self.line_begin("x", x_lat)
+            self.line_y.wait_recv()
+            self.line_begin("y", y_lat)
+
+        def line_far(self):
+            if not self.line_taps:
+                return
+            self.line_d.wait_recv()
+            self.line_begin("d", d_lat)
+
+        def line_pass(self, name, lat_id, step):
+            @pl.when(q >= step)
+            def _():
+                self.going_up[name, step].wait_recv()
+
+            self.line_up(name, lat_id, step)
+
+            @pl.when(q < n_q - step)
+            def _():
+                self.going_down[name, step].wait_recv()
+
+            self.line_down(name, lat_id, step)
+
+        def line_step(self, step, names=("own", "x", "y", "d")):
+            if not self.line_taps or step >= n_q:
+                return
+            for name in names:
+                self.line_pass(name, {"own": lat, "x": x_lat, "y": y_lat, "d": d_lat}[name], step)
+
+        def core_copy(self, lat_id, k, low, high):
+            if not self.has_rest:
+                return
+            self.to_core.append(self.give(lat_id, z_ids[k], low, high, partner))
+
+        def start_z(self):
+            if not self.has_rest:
+                return
+            for k in range(1, n_q):
+                self.to_z[k] = self.give(lat, q, 0, width, z_peers[k - 1])
+
+        def spread_x(self, k):
+            if not self.has_rest:
+                return
+            self.to_x[k] = self.give(lat, z_ids[k], 0, width, x_peer)
+
+        def spread_y(self, k):
+            if not self.has_rest:
+                return
+            self.to_y[k] = self.give(lat, z_ids[k], 0, width, y_peer)
+
+        def from_z(self, k):
+            if not self.has_rest:
+                return
+            self.to_z[k].wait_recv()
+
+        def relay_x(self, k):
+            if not self.has_rest:
+                return
+            self.to_x[k].wait_recv()
+            self.diag_y[k] = self.give(x_lat, z_ids[k], 0, self.cut, y_peer)
+            self.core_copy(x_lat, k, 0, width)
+
+        def relay_y(self, k):
+            if not self.has_rest:
+                return
+            self.to_y[k].wait_recv()
+            if self.cut < width:
+                self.diag_x[k] = self.give(y_lat, z_ids[k], self.cut, width, x_peer)
+            self.core_copy(y_lat, k, 0, width)
+
+        def close(self, k):
+            if not self.has_rest:
+                return
+            self.diag_y[k].wait_recv()
+            self.core_copy(d_lat, k, 0, self.cut)
+            if self.cut < width:
+                self.diag_x[k].wait_recv()
+                self.core_copy(d_lat, k, self.cut, width)
+
+        def finish(self):
+            for copy in self.to_core:
+                copy.wait_recv()
+            for condition, copy in self.line_core:
+                @pl.when(condition)
+                def _(copy=copy):
+                    copy.wait_recv()
+
+    def edges(field):
+        to_west = send(fields.at[field, 1], fields.at[field, cols + 1], west)
+        to_east = send(fields.at[field, cols], fields.at[field, 0], east)
+        return to_west, to_east
+
+    def last_row(index):
+        return lax.rem(index, lat_rows) == lat_rows - 1
+
+    def first_row(index):
+        return lax.rem(index, lat_rows) == 0
+
+    take = [
+        selector((halo_rows, span), lambda m, n: n == m * lat_rows),
+        selector((halo_rows, span), lambda m, n: n == m * lat_rows + lat_rows - 1),
+    ]
+    for copy in up_load:
+        copy.wait()
+
+    @pl.loop(0, chunks)
+    def _(c):
+        fields[1, pl.ds(1 + c * chunk, chunk)] = up_raw[pl.ds(c * chunk, chunk)].reshape(
+            chunk, group_rows, width
+        )
+
+    pl.semaphore_wait(barrier, len(greeted))
+    side_edges = {1: edges(1)}
+    old = Gather(w_old, width, OLD_LINE_TAPS)
+    old.line_start()
+    old.start_z()
+    old.core_copy(lat, 0, 0, width)
+    @pl.loop(0, chunks)
+    def _(c):
+        block = fields[1, pl.ds(1 + c * chunk, chunk)].reshape(span, width)
+        for side in range(2):
+            halo_out[side, c] = jnp.dot(
+                take[side], block, preferred_element_type=jnp.float32
+            ).astype(jnp.bfloat16)
+
+
+    near = chunks - chunks // 2
+    has_above, has_below = lat > 0, lat < n_lat - 1
+    inner = jnp.logical_and(has_above, has_below)
+    outer = jnp.logical_not(inner)
+    goes_up = lax.rem(lat, 2) == 1
+    parts = (pl.ds(0, near), pl.ds(near, chunks - near))
+
+    def halo_copy(side, part_index, target):
+        piece = parts[part_index]
+        return remote(
+            halo_out.at[side, piece], halo_in.at[side, piece], target, slots(1)
+        )
+
+    x_side = jnp.where(goes_up, 0, 1)
+    x_halo = [halo_copy(x_side, index, x_peer) for index in range(2)]
+    d_halo = halo_copy(1 - x_side, 0, d_peer)
+    y_halo = remote(
+        halo_out.at[1 - x_side, parts[1]], halo_pass, y_peer, slots(1)
+    )
+    passed = remote(
+        halo_pass, halo_in.at[1 - x_side, parts[1]], x_peer, slots(1)
+    )
+
+    @pl.when(inner)
+    def _():
+        y_halo.start()
+
+    x_halo[0].start()
+    x_halo[1].start()
+
+    @pl.when(inner)
+    def _():
+        d_halo.start()
+
+    old.line_start_y()
+    old.spread_y(0)
+    for copy in act_load:
+        copy.wait()
+
+    @pl.loop(0, chunks)
+    def _(c):
+        acts[pl.ds(c * span, span)] = act_raw[pl.ds(c * chunk, chunk)].reshape(span, width)
+
+    part_slot = slots(taps)
+
+    def part_copy(tap):
+        return remote(
+            part.at[tap, :, :, 1 - core], core_in.at[tap], partner, part_slot + tap
+        )
+
+    first_copies, second_copies, third_copies = {}, {}, {}
+
+    order = (4, 3, 5, 1, 7, 0, 2, 6, 8)
+
+    def reduce_tap(slot, cut):
+        part_copy(slot).wait_recv()
+        for k in range(n_q):
+            def total(lat_id):
+                return part[slot, lat_id, k, core] + core_in[slot, lat_id, k]
+
+            mine[slot, k] = total(lat)
+            first[slot, 1, k] = total(d_lat).astype(jnp.bfloat16)
+            from_x, from_y = total(x_lat), total(y_lat)
+            first[slot, 0, k, :, :cut] = from_y[:, :cut].astype(jnp.bfloat16)
+            keep[slot, k, :, :cut] = from_x[:, :cut]
+            if cut < width:
+                first[slot, 0, k, :, cut:] = from_x[:, cut:].astype(jnp.bfloat16)
+                keep[slot, k, :, cut:] = from_y[:, cut:]
+
+    def weight_tap(slot):
+        r, s = divmod(order[slot], 3)
+        shifted = fields[r, pl.ds(2 - s, cols)].reshape(cols * group_rows, width)
+        part[slot] = lax.dot_general(
+            acts[...], shifted, (((0,), (0,)), ((), ())), preferred_element_type=jnp.float32,
+        ).reshape(n_lat, n_q, 2, rows, width)
+        part_copy(slot).start()
+
+    def reduce_first(unit):
+        low_slot, high_slot, cut = unit
+        piece = pl.ds(low_slot, high_slot - low_slot)
+        copies = {0: [], 1: []}
+        for slot in (1, 0):
+            for target, low, high in ((y_peer, 0, cut), (x_peer, cut, width)):
+                if low < high:
+                    lanes = pl.ds(low, high - low)
+                    copies[slot].append(send(
+                        first.at[piece, slot, :, :, lanes],
+                        first_in.at[piece, slot, :, :, lanes], target,
+                    ))
+        first_copies[unit] = copies
+
+    def reduce_second(unit):
+        low_slot, high_slot, cut = unit
+        for copy in first_copies[unit][1]:
+            copy.wait_recv()
+
+        @pl.loop(low_slot, high_slot)
+        def _(tap):
+            for k in range(n_q):
+                second[tap, k] = (
+                    keep[tap, k] + first_in[tap, 1, k].astype(jnp.float32)
+                ).astype(jnp.bfloat16)
+
+        piece = pl.ds(low_slot, high_slot - low_slot)
+        second_copies[unit] = []
+        for target, low, high in ((x_peer, 0, cut), (y_peer, cut, width)):
+            if low < high:
+                lanes = pl.ds(low, high - low)
+                second_copies[unit].append(send(
+                    second.at[piece, :, :, lanes], second_in.at[piece, :, :, lanes], target
+                ))
+
+    def reduce_third(unit):
+        low_slot, high_slot, _ = unit
+        for copy in first_copies[unit][0] + second_copies[unit]:
+            copy.wait_recv()
+
+        @pl.loop(low_slot, high_slot)
+        def _(tap):
+            for k in range(n_q):
+                block = z_ids[k]
+                total = (
+                    mine[tap, block] + first_in[tap, 0, block].astype(jnp.float32)
+                    + second_in[tap, block].astype(jnp.float32)
+                )
+                if k == 0:
+                    mine[tap, block] = total
+                else:
+                    last_out[k - 1, tap] = total.astype(jnp.bfloat16)
+
+        piece = pl.ds(low_slot, high_slot - low_slot)
+        third_copies[unit] = [
+            send(last_out.at[k - 1, piece], last_in.at[k - 1, piece], z_peers[k - 1])
+            for k in range(1, n_q)
+        ]
+
+    def input_piece(index):
+        total = None
+        for tap in range(taps):
+            r, s = divmod(tap, 3)
+            shifted = fields[r, pl.ds(index * chunk + 2 - s, chunk)]
+            product = lax.dot_general(
+                shifted.reshape(span, width), w_old[tap].reshape(-1, width),
+                (((1,), (1,)), ((), ())), preferred_element_type=jnp.float32,
+            )
+            total = product if total is None else total + product
+        total = total.reshape(chunk, group_rows, width)
+        for b in range(batch):
+            input_grad[b, pl.ds(index * chunk, chunk)] = total[
+                :, b * lat_rows : (b + 1) * lat_rows
+            ].astype(jnp.bfloat16)
+
+    def input_pieces(low, high):
+        @pl.loop(low, high)
+        def _(index):
+            input_piece(index)
+
+    units = [(0, 3, width), (3, 5, half), (5, 7, half), (7, 9, half)]
+    weight_tap(0)
+    for copy in side_edges[1]:
+        copy.wait_recv()
+    weight_tap(1)
+    reduce_tap(0, width)
+    weight_tap(2)
+    reduce_tap(1, width)
+    reduce_tap(2, width)
+    reduce_first(units[0])
+    @pl.when(outer)
+    def _():
+        y_halo.wait_recv()
+        passed.start()
+
+    old.line_cross()
+    old.line_step(1, ("own",))
+    for copy in x_halo:
+        copy.wait_recv()
+
+    @pl.when(inner)
+    def _():
+        d_halo.wait_recv()
+        passed.wait_recv()
+
+    @pl.when(jnp.logical_not(has_below))
+    def _():
+        halo_in[0] = jnp.zeros(halo_in.shape[1:], halo_in.dtype)
+
+    @pl.when(jnp.logical_not(has_above))
+    def _():
+        halo_in[1] = jnp.zeros(halo_in.shape[1:], halo_in.dtype)
+
+    shift = [
+        selector((span, span), lambda m, n: jnp.logical_and(n == m + 1, jnp.logical_not(last_row(m)))),
+        selector((span, span), lambda m, n: jnp.logical_and(n == m - 1, jnp.logical_not(first_row(m)))),
+    ]
+    place = [
+        selector((span, halo_rows), lambda m, n: jnp.logical_and(n == m // lat_rows, last_row(m))),
+        selector((span, halo_rows), lambda m, n: jnp.logical_and(n == m // lat_rows, first_row(m))),
+    ]
+
+    @pl.loop(0, chunks)
+    def _(c):
+        block = fields[1, pl.ds(1 + c * chunk, chunk)].reshape(span, width)
+        for side in range(2):
+            moved = jnp.dot(shift[side], block, preferred_element_type=jnp.float32)
+            moved = moved + jnp.dot(
+                place[side], halo_in[side, c], preferred_element_type=jnp.float32
+            )
+            fields[2 * side, pl.ds(1 + c * chunk, chunk)] = moved.astype(jnp.bfloat16).reshape(
+                chunk, group_rows, width
+            )
+
+    side_edges[0], side_edges[2] = edges(0), edges(2)
+    old.line_step(1, ("x", "y"))
+    old.line_step(2, ("own",))
+    weight_tap(3)
+    weight_tap(4)
+    reduce_second(units[0])
+    reduce_tap(3, half)
+    reduce_tap(4, half)
+    reduce_first(units[1])
+    old.line_far()
+    old.line_step(2, ("x", "y"))
+    old.line_step(3, ("own",))
+    for copy in side_edges[0] + side_edges[2]:
+        copy.wait_recv()
+    weight_tap(5)
+    weight_tap(6)
+    reduce_tap(5, half)
+    reduce_tap(6, half)
+    reduce_first(units[2])
+    old.line_step(1, ("d",))
+    old.line_step(3, ("x", "y"))
+    weight_tap(7)
+    weight_tap(8)
+    reduce_tap(7, half)
+    reduce_tap(8, half)
+    reduce_first(units[3])
+    old.line_step(2, ("d",))
+    reduce_second(units[1])
+    reduce_third(units[0])
+    reduce_second(units[2])
+    reduce_third(units[1])
+    reduce_second(units[3])
+    for k in range(1, n_q):
+        old.from_z(k)
+        old.spread_y(k)
+        old.core_copy(lat, k, 0, width)
+    for k in range(n_q):
+        old.spread_x(k)
+    reduce_third(units[2])
+    reduce_third(units[3])
+    for k in range(n_q):
+        old.relay_y(k)
+        old.relay_x(k)
+    old.line_step(3, ("d",))
+    for step in range(4, n_q):
+        old.line_step(step)
+    for unit in units:
+        for copy in third_copies[unit]:
+            copy.wait_recv()
+    square = jnp.zeros((rows, width), jnp.float32)
+    for index, tap in enumerate(order):
+        grad = mine[index, q]
+        for k in range(n_q - 1):
+            grad = grad + last_in[k, index].astype(jnp.float32)
+        clipped[tap] = grad
+        square = square + grad * grad
+    square = jnp.sum(square)
+    slot = 0
+    fill = [chunks // 2, chunks // 6]
+    done = 0
+    for stage, peers in enumerate(([partner] + z_peers + z_twins, [x_peer, y_peer, d_peer])):
+        norm_out[stage] = jnp.full(norm_out.shape[1:], square, jnp.float32)
+        copies = []
+        for index, target in enumerate(peers):
+            copies.append(send(norm_out.at[stage], norm_in.at[slot + index], target))
+        if stage == 0:
+            for k in range(n_q):
+                old.close(k)
+            old.finish()
+        input_pieces(done, done + fill[stage])
+        done += fill[stage]
+        tile = norm_out[stage]
+        for index, copy in enumerate(copies):
+            copy.wait_recv()
+            tile = tile + norm_in[slot + index]
+        slot += len(peers)
+        square = jnp.max(tile)
+    one_load.wait()
+    two_load.wait()
+    square = jnp.full((1, 1), square, jnp.float32)
+    clip_factor = jnp.minimum(1.0, max_norm / (jnp.sqrt(square) + norm_eps))
+
+    @pl.loop(0, taps)
+    def _(tap):
+        scaled = clip_factor * clipped[tap]
+        clipped[tap] = scaled
+        moment = beta_one * one[tap] + (1.0 - beta_one) * scaled
+        spread = beta_two * two[tap] + (1.0 - beta_two) * scaled * scaled
+        new_one[tap] = moment
+        new_two[tap] = spread
+        first_hat = moment / (1.0 - beta_one**step_count)
+        second_hat = spread / (1.0 - beta_two**step_count)
+        updated = master[tap] - learn_rate * (
+            first_hat / (jnp.sqrt(second_hat) + adam_eps) + decay_rate * master[tap]
+        )
+        new_master[tap] = updated
+        w_new[tap, lat, q, core] = updated.astype(jnp.bfloat16)
+
+    new = Gather(w_new, half, NEW_LINE_TAPS)
+    new.line_start()
+    new.line_start_y()
+    new.start_z()
+    new.spread_x(0)
+    new.spread_y(0)
+    new.core_copy(lat, 0, 0, width)
+    input_pieces(done, chunks)
+    new.line_cross()
+    for k in range(1, n_q):
+        new.from_z(k)
+        new.spread_x(k)
+        new.spread_y(k)
+        new.core_copy(lat, k, 0, width)
+        new.relay_x(k - 1)
+        new.relay_y(k - 1)
+        if k == 1:
+            new.line_far()
+        new.line_step(k)
+    new.relay_x(n_q - 1)
+    new.relay_y(n_q - 1)
+    for k in range(n_q):
+        new.close(k)
+    new.finish()
+
+    for copy in x_halo:
+        copy.wait_send()
+
+    @pl.when(inner)
+    def _():
+        y_halo.wait_send()
+        d_halo.wait_send()
+
+    @pl.when(outer)
+    def _():
+        passed.wait_send()
+
+    @pl.loop(0, taps)
+    def _(tap):
+        part_copy(tap).wait_send()
+
+    for copy in pending:
+        copy.wait_send()
+    for condition, copy in guarded:
+        @pl.when(condition)
+        def _(copy=copy):
+            copy.wait_send()
+
+
+def land(*refs):
+    count = len(refs) // 2
+    sources, targets, sem = refs[:count], refs[count : 2 * count], refs[-1]
+    copies = [
+        pltpu.make_async_copy(source, target, sem.at[index])
+        for index, (source, target) in enumerate(zip(sources, targets))
+    ]
+    for copy in copies:
+        copy.start()
+    for copy in copies:
+        copy.wait()
+
+
+def landed(arrays):
+    anywhere = pl.BlockSpec(memory_space=pl.ANY)
+    return pl.pallas_call(
+        land,
+        out_shape=tuple(jax.ShapeDtypeStruct(a.shape, a.dtype) for a in arrays),
+        in_specs=[anywhere] * len(arrays),
+        out_specs=(anywhere,) * len(arrays),
+        scratch_shapes=[pltpu.SemaphoreType.DMA((len(arrays),))],
+        compiler_params=pltpu.CompilerParams(vmem_limit_bytes=1024 * 1024),
+        name="land",
+    )(*arrays)
+
+
+def fused_step(up, act, master, one, two):
+    n_lat, n_q = lax.axis_size("lat"), lax.axis_size("lon") // 2
+    taps, rows, width = master.shape
+    batch, cols, lat_rows, _ = up.shape
+    group_rows = batch * lat_rows
+    chunk = max(c for c in range(1, 17) if cols % c == 0)
+    chunks = cols // chunk
+    halo_rows = -(-chunk * batch // ROW_TILE) * ROW_TILE
+    max_norm = math.sqrt(float(n_lat * n_q * 2 * taps * rows * width))
+    bf16, f32 = jnp.bfloat16, jnp.float32
+    shard = pltpu.VMEM(master.shape, f32)
+    whole = (taps, n_lat, n_q, 2, rows, width)
+    lat_block = (taps, n_q, rows, width)
+    vmem, hbm = (pl.BlockSpec(memory_space=m) for m in (pltpu.VMEM, pltpu.HBM))
+    peers = 2 * n_q + n_lat - 2
+    copies = 192 + 32 * (n_q + n_lat)
+    return pl.pallas_call(
+        functools.partial(whole_step, n_lat, n_q, max_norm),
+        out_shape=(
+            pltpu.VMEM(up.shape, bf16), pltpu.VMEM(whole, bf16), shard, shard, shard, shard,
+        ),
+        in_specs=[hbm] * 5,
+        out_specs=(vmem,) * 6,
+        scratch_shapes=[
+            pltpu.VMEM(master.shape, f32),
+            pltpu.VMEM(master.shape, f32),
+            pltpu.VMEM(master.shape, f32),
+            pltpu.VMEM((cols, batch, lat_rows, width), bf16),
+            pltpu.VMEM((cols, batch, lat_rows, width), bf16),
+            pltpu.VMEM((cols * group_rows, width), bf16),
+            pltpu.VMEM((3, cols + 2, group_rows, width), bf16),
+            pltpu.VMEM((2, chunks, halo_rows, width), bf16),
+            pltpu.VMEM((2, chunks, halo_rows, width), bf16),
+            pltpu.VMEM((chunks // 2, halo_rows, width), bf16),
+            pltpu.VMEM(whole, bf16),
+            pltpu.VMEM(whole, f32),
+            pltpu.VMEM((taps, n_lat, n_q, rows, width), f32),
+            pltpu.VMEM(lat_block, f32),
+            pltpu.VMEM(lat_block, f32),
+            pltpu.VMEM((taps, 2, n_q, rows, width), bf16),
+            pltpu.VMEM((taps, 2, n_q, rows, width), bf16),
+            pltpu.VMEM(lat_block, bf16),
+            pltpu.VMEM(lat_block, bf16),
+            pltpu.VMEM((n_q - 1, taps, rows, width), bf16),
+            pltpu.VMEM((n_q - 1, taps, rows, width), bf16),
+            pltpu.VMEM((3, 8, LANE_TILE), f32),
+            pltpu.VMEM((peers, 8, LANE_TILE), f32),
+            pltpu.SemaphoreType.DMA((2 * batch + 3,)),
+            pltpu.SemaphoreType.DMA((copies,)),
+            pltpu.SemaphoreType.DMA((copies,)),
+        ],
+        compiler_params=pltpu.CompilerParams(
+            collective_id=2, has_side_effects=True, vmem_limit_bytes=48 * 1024 * 1024
+        ),
+        name="whole_step",
+    )(up, act, master, one, two)
+
+
+def takes_fused(activations, master):
+    n_lat, n_q = lax.axis_size("lat"), lax.axis_size("lon") // 2
+    batch, lat_rows, cols, _ = activations.shape
+    return (
+        n_lat == 4 and n_q & (n_q - 1) == 0 and n_q > 1 and master.shape[0] % ROW_TILE == 0
+        and (batch * lat_rows) % ROW_TILE == 0 and cols % 2 == 0
+        and master.shape[2] % (2 * LANE_TILE) == 0 and master.shape[1] == 9
+    )
+
+
 def per_device(activations, upstream, master, moment_one, moment_two):
+    if not takes_fused(activations, master):
+        return per_device_general(activations, upstream, master, moment_one, moment_two)
+
+    def by_col(field):
+        return jnp.transpose(field, (0, 2, 1, 3))
+
+    def by_tap(array):
+        return jnp.transpose(array, (1, 0, 2))
+
+    input_grad, gathered, new_master, new_one, new_two, clipped = landed(fused_step(
+        by_col(upstream), by_col(activations), by_tap(master), by_tap(moment_one),
+        by_tap(moment_two),
+    ))
+    new_weights = by_tap(gathered.reshape(gathered.shape[0], -1, gathered.shape[-1]))
+    return (
+        by_col(input_grad), new_weights, by_tap(new_master), by_tap(new_one), by_tap(new_two),
+        by_tap(clipped),
+    )
+
+
+def per_device_general(activations, upstream, master, moment_one, moment_two):
     lat_rows = activations.shape[1]
     lon_cols = activations.shape[2]
     grad_flat = upstream.reshape(-1, upstream.shape[3])

time: 241 us -> 105 us (0.44)
  Pallas kernels: 166 us -> 104 us
  matrix products: 28.8 us -> 0 us
  local copies, waits for them, and re-layouts: 22.8 us -> 0 us
  between operations: 14.4 us -> 0.8 us
  other arithmetic: 8.73 us -> 0 us
    pallas_call x2, Pallas kernels: 166 us -> 104 us  [the longest x1 101 us: fused_step(): pl.pallas_call(functools.partial(whole_step, n_lat, n_q, max_norm), out_s...]
    dot_general x9 -> x0, matrix products: 18.3 us -> none  [input_compute(): lax.dot_general(tap_slab, grad_flat, (((0,), (0,)), ((), ())), preferred_...]
    conv_general_dilated x1 -> x0, matrix products: 10.5 us -> none  [per_device(): lax.conv_general_dilated(grad_wide, old_full.reshape(old_full.shape[0], 3...]
    unnamed x29 -> x0, local copies, waits for them, and re-layouts: 10.3 us -> none
    transpose x1 -> x0, local copies, waits for them, and re-layouts: 5.32 us -> none  [per_device(): jnp.transpose(gathered, (2, 1, 0, 4, 3, 5))]
    select_n x1 -> x0, other arithmetic: 4.55 us -> none  [mask_poles(): jnp.where(jnp.logical_or(upper, lower), jnp.zeros((), wide_field.dtype),...]
    convert_element_type x2 -> x0, local copies, waits for them, and re-layouts: 2.83 us -> none  [per_device(): input_grad = lax.conv_general_dilated(grad_wide, old_full.reshape(old_ful...]
    conv_general_dilated x1 -> x0, other arithmetic: 2.71 us -> none  [per_device(): lax.conv_general_dilated(grad_wide, old_full.reshape(old_full.shape[0], 3...]
  transfers between devices with their start and end apart: 1 -> 0, of which waited for: 0 -> 0; matrix products, arithmetic and copies ran while one was open for 17% -> 0% of each run, Pallas kernels for 69% -> 0%
where the time goes in v2:
time: 105 us
  Pallas kernels  104 us (99%)
    pallas_call x1, Pallas kernels, fused_step(): pl.pallas_call(functools.partial(whole_step, n_lat, n_q, max_norm), out_s...  101 us
    pallas_call x1, Pallas kernels, landed(): pl.pallas_call(land, out_shape=tuple((jax.ShapeDtypeStruct(a.shape, a.dty...  3.07 us

profile of v2, /device:TPU:0, one launch (start us, length us, event | category | flops | bytes accessed | tf_op | source)
XLA Modules:
  0.0 104.7 jit_solution(764357333524609105)
XLA Ops:
  0.6 100.8 %whole_step.1 = (bf16[4,90,4,512]{3,2,1,0:T(4,128)(2,1)S(1)}, bf16[9,4,4,2,16,512]{5,4,3,2,1,0:T(8,128)(2,1)S(1)}, f32[9,16,512]{2,1,0:T(8,128)S(1)}, f32[9,16,5...) custom-call(bf16[4,90,4,512]{3,2,1,0:T(4,128)(2,1)} %bitcast.13, ...), custom_call_target="tpu_custom_call" | custom-call | tf_op jit(solution)/shard_map/whole_step/pallas_call | solution.py:1062
  101.5 3.1 %land.1 = (bf16[4,90,4,512]{3,2,1,0:T(4,128)(2,1)}, bf16[9,4,4,2,16,512]{5,4,3,2,1,0:T(8,128)(2,1)}, f32[9,16,512]{2,1,0:T(8,128)}, f32[9,16,512]{2,1,0:T(8,128)...) custom-call(bf16[4,90,4,512]{3,2,1,0:T(4,128)(2,1)S(1)} %get-tuple-element.18.refs_0_, ...), custom_call_target="tpu_custom_call" | custom-call | tf_op jit(solution)/shard_map/land/pallas_call | solution.py:1035

commit v3 on v2

--- a/solution.py
+++ b/solution.py
@@ -383,8 +383,6 @@
     chunk = cols // chunks
     span = chunk * group_rows
     half = width // 2
-    counter = [0]
-    pending, guarded = [], []
 
     def at(lat_id, q_id, core_id):
         return (lat_id, q_id * 2 + core_id)
@@ -413,32 +411,29 @@
     above = (jnp.maximum(lat - 1, 0), lon)
     below = (jnp.minimum(lat + 1, n_lat - 1), lon)
 
-    def slots(count):
-        start = counter[0]
-        counter[0] += count
-        return start
-
-    def remote(src, dst, target, index):
+    used = [0, 0]
+    closing = []
+
+    def remote(src, dst, target, sent, landed_at):
         return pltpu.make_async_remote_copy(
-            src_ref=src, dst_ref=dst, send_sem=send_sem.at[index],
-            recv_sem=recv_sem.at[index], device_id=target, device_id_type=MESH,
+            src_ref=src, dst_ref=dst, send_sem=send_sem.at[sent],
+            recv_sem=recv_sem.at[landed_at], device_id=target, device_id_type=MESH,
         )
 
-    def send(src, dst, target):
-        copy = remote(src, dst, target, slots(1))
-        copy.start()
-        pending.append(copy)
-        return copy
-
-    def send_if(condition, src, dst, target):
-        copy = remote(src, dst, target, slots(1))
-
-        @pl.when(condition)
-        def _():
-            copy.start()
-
-        guarded.append((condition, copy))
-        return copy
+    def landing(count=1):
+        used[1] += count
+        return used[1] - count
+
+    def outgoing(view, condition=None):
+        used[0] += 1
+        closing.append((condition, remote(view, view, partner, used[0] - 1, 0)))
+        return used[0] - 1
+
+    def arrived(view, landed_at):
+        remote(view, view, partner, 0, landed_at).wait_recv()
+
+    def send(src, dst, target, sent, landed_at):
+        remote(src, dst, target, sent, landed_at).start()
 
     barrier = pltpu.get_barrier_semaphore()
     greeted = [partner, x_peer, y_peer, d_peer] + z_peers + z_twins
@@ -469,161 +464,177 @@
 
     class Gather:
         def __init__(self, buffer, cut, line_taps):
-            self.buffer, self.cut = buffer, cut
-            self.line_taps = line_taps
+            self.buffer, self.cut, self.line_taps = buffer, cut, line_taps
             self.line = pl.ds(0, line_taps)
             self.rest = pl.ds(line_taps, taps - line_taps)
             self.has_rest = line_taps < taps
-            self.line_x = self.line_y = self.line_d = None
-            self.going_up, self.going_down, self.line_core = {}, {}, []
-            self.to_z, self.to_x, self.to_y, self.to_core = {}, {}, {}, []
-            self.diag_x, self.diag_y = {}, {}
-
-        def give(self, lat_id, q_id, low, high, target):
-            piece = self.buffer.at[
+            self.core_sent = outgoing(buffer.at[:, :, :, core])
+            self.core_landed = landing()
+            self.sent, self.landed = {}, {}
+            if self.has_rest:
+                for name, view in (
+                    ("z", buffer.at[self.rest, lat, pl.ds(0, n_q - 1), core]),
+                    ("x", buffer.at[self.rest, lat, :, core]),
+                    ("y", buffer.at[self.rest, lat, :, core]),
+                    ("low", buffer.at[self.rest, x_lat, :, core, :, pl.ds(0, cut)]),
+                ):
+                    self.sent[name], self.landed[name] = outgoing(view), landing(n_q)
+                if cut < width:
+                    lanes = pl.ds(cut, width - cut)
+                    self.sent["high"] = outgoing(
+                        buffer.at[self.rest, y_lat, :, core, :, lanes]
+                    )
+                    self.landed["high"] = landing(n_q)
+            if line_taps:
+                for name in ("line_x", "line_y", "line_d"):
+                    self.sent[name] = outgoing(self.line_block(lat, q))
+                    self.landed[name] = landing()
+                for step in range(n_q - 1):
+                    plane = buffer.at[self.line, :, q, core]
+                    self.sent["up", step] = outgoing(
+                        plane, jnp.logical_and(q >= step, q < n_q - 1)
+                    )
+                    self.sent["down", step] = outgoing(
+                        plane, jnp.logical_and(q < n_q - step, q > 0)
+                    )
+                    for name in ("own", "xy", "d"):
+                        self.landed["up", name, step + 1] = landing()
+                        self.landed["down", name, step + 1] = landing()
+
+        def block(self, lat_id, q_id, low, high):
+            return self.buffer.at[
                 self.rest, lat_id, q_id, core, :, pl.ds(low, high - low)
             ]
-            return send(piece, piece, target)
+
+        def give(self, name, k, lat_id, q_id, low, high, target):
+            piece = self.block(lat_id, q_id, low, high)
+            send(piece, piece, target, self.sent[name], self.landed[name] + k)
+
+        def take(self, name, k, low, high):
+            arrived(self.block(lat, q, low, high), self.landed[name] + k)
+
+        def core_copy(self, lat_id, k, low, high):
+            if self.has_rest:
+                piece = self.block(lat_id, z_ids[k], low, high)
+                send(piece, piece, partner, self.core_sent, self.core_landed)
 
         def line_block(self, lat_id, q_id):
             return self.buffer.at[self.line, lat_id, q_id, core]
 
-        def line_give(self, lat_id, target):
+        def line_give(self, name, lat_id, target):
             piece = self.line_block(lat_id, q)
-            return send(piece, piece, target)
-
-        def line_up(self, name, lat_id, step):
-            block = jnp.maximum(q - step, 0)
-            piece = self.line_block(lat_id, block)
-            here = q >= step
-            self.going_up[name, step + 1] = send_if(
-                jnp.logical_and(here, q < n_q - 1), piece, piece, next_z
-            )
-            if step:
-                self.line_core.append((here, send_if(here, piece, piece, partner)))
-
-        def line_down(self, name, lat_id, step):
-            block = jnp.minimum(q + step, n_q - 1)
-            piece = self.line_block(lat_id, block)
-            here = q < n_q - step
-            self.going_down[name, step + 1] = send_if(
-                jnp.logical_and(here, q > 0), piece, piece, last_z
-            )
-            if step:
-                self.line_core.append((here, send_if(here, piece, piece, partner)))
-
-        def line_begin(self, name, lat_id):
-            self.line_up(name, lat_id, 0)
-            self.line_down(name, lat_id, 0)
-            self.to_core.append(self.line_give(lat_id, partner))
-
-        def line_start(self):
-            if not self.line_taps:
-                return
-            self.line_x = self.line_give(lat, x_peer)
-            self.line_begin("own", lat)
-
-        def line_start_y(self):
-            if not self.line_taps:
-                return
-            self.line_y = self.line_give(lat, y_peer)
-
-        def line_cross(self):
-            if not self.line_taps:
-                return
-            self.line_x.wait_recv()
-            self.line_d = self.line_give(x_lat, y_peer)
-            self.line_begin("x", x_lat)
-            self.line_y.wait_recv()
-            self.line_begin("y", y_lat)
-
-        def line_far(self):
-            if not self.line_taps:
-                return
-            self.line_d.wait_recv()
-            self.line_begin("d", d_lat)
-
-        def line_pass(self, name, lat_id, step):
-            @pl.when(q >= step)
-            def _():
-                self.going_up[name, step].wait_recv()
-
-            self.line_up(name, lat_id, step)
-
-            @pl.when(q < n_q - step)
-            def _():
-                self.going_down[name, step].wait_recv()
-
-            self.line_down(name, lat_id, step)
-
-        def line_step(self, step, names=("own", "x", "y", "d")):
+            send(piece, piece, target, self.sent[name], self.landed[name])
+
+        def line_take(self, name):
+            arrived(self.line_block(lat, q), self.landed[name])
+
+        def line_core(self, lat_id, q_id):
+            piece = self.line_block(lat_id, q_id)
+            send(piece, piece, partner, self.core_sent, self.core_landed)
+
+        def line_pass(self, name, lat_ids, step):
+            for way, here, ahead, block, target in (
+                ("up", q >= step, q < n_q - 1, jnp.maximum(q - step, 0), next_z),
+                ("down", q < n_q - step, q > 0, jnp.minimum(q + step, n_q - 1), last_z),
+            ):
+                if step:
+                    @pl.when(here)
+                    def _():
+                        view = self.buffer.at[self.line, pl.ds(0, len(lat_ids)), q, core]
+                        arrived(view, self.landed[way, name, step])
+                        for lat_id in lat_ids:
+                            self.line_core(lat_id, block)
+
+                if step < n_q - 1:
+                    @pl.when(jnp.logical_and(here, ahead))
+                    def _():
+                        for lat_id in lat_ids:
+                            piece = self.line_block(lat_id, block)
+                            send(
+                                piece, piece, target, self.sent[way, step],
+                                self.landed[way, name, step + 1],
+                            )
+
+        def line_step(self, step, names=("own", "xy", "d")):
             if not self.line_taps or step >= n_q:
                 return
             for name in names:
-                self.line_pass(name, {"own": lat, "x": x_lat, "y": y_lat, "d": d_lat}[name], step)
-
-        def core_copy(self, lat_id, k, low, high):
-            if not self.has_rest:
-                return
-            self.to_core.append(self.give(lat_id, z_ids[k], low, high, partner))
+                lat_ids = {"own": (lat,), "xy": (x_lat, y_lat), "d": (d_lat,)}[name]
+                self.line_pass(name, lat_ids, step)
+
+        def line_start(self):
+            if self.line_taps:
+                self.line_give("line_x", lat, x_peer)
+                self.line_step(0, ("own",))
+                self.line_core(lat, q)
+
+        def line_start_y(self):
+            if self.line_taps:
+                self.line_give("line_y", lat, y_peer)
+
+        def line_cross(self):
+            if self.line_taps:
+                self.line_take("line_x")
+                self.line_give("line_d", x_lat, y_peer)
+                self.line_core(x_lat, q)
+                self.line_take("line_y")
+                self.line_core(y_lat, q)
+                self.line_step(0, ("xy",))
+
+        def line_far(self):
+            if self.line_taps:
+                self.line_take("line_d")
+                self.line_core(d_lat, q)
+                self.line_step(0, ("d",))
 
         def start_z(self):
-            if not self.has_rest:
-                return
-            for k in range(1, n_q):
-                self.to_z[k] = self.give(lat, q, 0, width, z_peers[k - 1])
+            if self.has_rest:
+                for k in range(1, n_q):
+                    self.give("z", k, lat, q, 0, width, z_peers[k - 1])
 
         def spread_x(self, k):
-            if not self.has_rest:
-                return
-            self.to_x[k] = self.give(lat, z_ids[k], 0, width, x_peer)
+            if self.has_rest:
+                self.give("x", k, lat, z_ids[k], 0, width, x_peer)
 
         def spread_y(self, k):
-            if not self.has_rest:
-                return
-            self.to_y[k] = self.give(lat, z_ids[k], 0, width, y_peer)
+            if self.has_rest:
+                self.give("y", k, lat, z_ids[k], 0, width, y_peer)
 
         def from_z(self, k):
-            if not self.has_rest:
-                return
-            self.to_z[k].wait_recv()
+            if self.has_rest:
+                self.take("z", k, 0, width)
 
         def relay_x(self, k):
-            if not self.has_rest:
-                return
-            self.to_x[k].wait_recv()
-            self.diag_y[k] = self.give(x_lat, z_ids[k], 0, self.cut, y_peer)
-            self.core_copy(x_lat, k, 0, width)
+            if self.has_rest:
+                self.take("x", k, 0, width)
+                self.give("low", k, x_lat, z_ids[k], 0, self.cut, y_peer)
+                self.core_copy(x_lat, k, 0, width)
 
         def relay_y(self, k):
-            if not self.has_rest:
-                return
-            self.to_y[k].wait_recv()
-            if self.cut < width:
-                self.diag_x[k] = self.give(y_lat, z_ids[k], self.cut, width, x_peer)
-            self.core_copy(y_lat, k, 0, width)
+            if self.has_rest:
+                self.take("y", k, 0, width)
+                if self.cut < width:
+                    self.give("high", k, y_lat, z_ids[k], self.cut, width, x_peer)
+                self.core_copy(y_lat, k, 0, width)
 
         def close(self, k):
-            if not self.has_rest:
-                return
-            self.diag_y[k].wait_recv()
-            self.core_copy(d_lat, k, 0, self.cut)
-            if self.cut < width:
-                self.diag_x[k].wait_recv()
-                self.core_copy(d_lat, k, self.cut, width)
+            if self.has_rest:
+                self.take("low", k, 0, self.cut)
+                self.core_copy(d_lat, k, 0, self.cut)
+                if self.cut < width:
+                    self.take("high", k, self.cut, width)
+                    self.core_copy(d_lat, k, self.cut, width)
 
         def finish(self):
-            for copy in self.to_core:
-                copy.wait_recv()
-            for condition, copy in self.line_core:
-                @pl.when(condition)
-                def _(copy=copy):
-                    copy.wait_recv()
+            arrived(self.buffer.at[:, :, :, 1 - core], self.core_landed)
+
+    edge_sent = outgoing(fields.at[0, pl.ds(0, 6)])
+    edge_landed = {1: landing(), 0: landing()}
 
     def edges(field):
-        to_west = send(fields.at[field, 1], fields.at[field, cols + 1], west)
-        to_east = send(fields.at[field, cols], fields.at[field, 0], east)
-        return to_west, to_east
+        landed_at = edge_landed[field % 2]
+        send(fields.at[field, 1], fields.at[field, cols + 1], west, edge_sent, landed_at)
+        send(fields.at[field, cols], fields.at[field, 0], east, edge_sent, landed_at)
 
     def last_row(index):
         return lax.rem(index, lat_rows) == lat_rows - 1
@@ -645,7 +656,7 @@
         )
 
     pl.semaphore_wait(barrier, len(greeted))
-    side_edges = {1: edges(1)}
+    edges(1)
     old = Gather(w_old, width, OLD_LINE_TAPS)
     old.line_start()
     old.start_z()
@@ -666,28 +677,28 @@
     goes_up = lax.rem(lat, 2) == 1
     parts = (pl.ds(0, near), pl.ds(near, chunks - near))
 
-    def halo_copy(side, part_index, target):
-        piece = parts[part_index]
-        return remote(
-            halo_out.at[side, piece], halo_in.at[side, piece], target, slots(1)
-        )
-
     x_side = jnp.where(goes_up, 0, 1)
-    x_halo = [halo_copy(x_side, index, x_peer) for index in range(2)]
-    d_halo = halo_copy(1 - x_side, 0, d_peer)
+    x_halo = remote(
+        halo_out.at[x_side], halo_in.at[x_side], x_peer, outgoing(halo_out.at[0]), landing()
+    )
+    d_halo = remote(
+        halo_out.at[1 - x_side, parts[0]], halo_in.at[1 - x_side, parts[0]], d_peer,
+        outgoing(halo_out.at[0, parts[0]], inner), landing(),
+    )
     y_halo = remote(
-        halo_out.at[1 - x_side, parts[1]], halo_pass, y_peer, slots(1)
+        halo_out.at[1 - x_side, parts[1]], halo_pass, y_peer, outgoing(halo_pass, inner),
+        landing(),
     )
     passed = remote(
-        halo_pass, halo_in.at[1 - x_side, parts[1]], x_peer, slots(1)
+        halo_pass, halo_in.at[1 - x_side, parts[1]], x_peer, outgoing(halo_pass, outer),
+        landing(),
     )
 
     @pl.when(inner)
     def _():
         y_halo.start()
 
-    x_halo[0].start()
-    x_halo[1].start()
+    x_halo.start()
 
     @pl.when(inner)
     def _():
@@ -702,14 +713,17 @@
     def _(c):
         acts[pl.ds(c * span, span)] = act_raw[pl.ds(c * chunk, chunk)].reshape(span, width)
 
-    part_slot = slots(taps)
+    part_sent, part_landed = outgoing(part.at[:, :, :, 1 - core]), landing(taps)
 
     def part_copy(tap):
         return remote(
-            part.at[tap, :, :, 1 - core], core_in.at[tap], partner, part_slot + tap
+            part.at[tap, :, :, 1 - core], core_in.at[tap], partner, part_sent,
+            part_landed + tap,
         )
 
-    first_copies, second_copies, third_copies = {}, {}, {}
+    first_sent, second_sent = outgoing(first), outgoing(second)
+    third_sent, third_landed = outgoing(last_out), landing()
+    first_landed, second_landed = {}, {}
 
     order = (4, 3, 5, 1, 7, 0, 2, 6, 8)
 
@@ -739,21 +753,21 @@
     def reduce_first(unit):
         low_slot, high_slot, cut = unit
         piece = pl.ds(low_slot, high_slot - low_slot)
-        copies = {0: [], 1: []}
         for slot in (1, 0):
+            first_landed[unit, slot] = landing()
             for target, low, high in ((y_peer, 0, cut), (x_peer, cut, width)):
                 if low < high:
                     lanes = pl.ds(low, high - low)
-                    copies[slot].append(send(
+                    send(
                         first.at[piece, slot, :, :, lanes],
-                        first_in.at[piece, slot, :, :, lanes], target,
-                    ))
-        first_copies[unit] = copies
+                        first_in.at[piece, slot, :, :, lanes], target, first_sent,
+                        first_landed[unit, slot],
+                    )
 
     def reduce_second(unit):
         low_slot, high_slot, cut = unit
-        for copy in first_copies[unit][1]:
-            copy.wait_recv()
+        piece = pl.ds(low_slot, high_slot - low_slot)
+        arrived(first_in.at[piece, 1], first_landed[unit, 1])
 
         @pl.loop(low_slot, high_slot)
         def _(tap):
@@ -762,19 +776,20 @@
                     keep[tap, k] + first_in[tap, 1, k].astype(jnp.float32)
                 ).astype(jnp.bfloat16)
 
-        piece = pl.ds(low_slot, high_slot - low_slot)
-        second_copies[unit] = []
+        second_landed[unit] = landing()
         for target, low, high in ((x_peer, 0, cut), (y_peer, cut, width)):
             if low < high:
                 lanes = pl.ds(low, high - low)
-                second_copies[unit].append(send(
-                    second.at[piece, :, :, lanes], second_in.at[piece, :, :, lanes], target
-                ))
+                send(
+                    second.at[piece, :, :, lanes], second_in.at[piece, :, :, lanes], target,
+                    second_sent, second_landed[unit],
+                )
 
     def reduce_third(unit):
         low_slot, high_slot, _ = unit
-        for copy in first_copies[unit][0] + second_copies[unit]:
-            copy.wait_recv()
+        piece = pl.ds(low_slot, high_slot - low_slot)
+        arrived(first_in.at[piece, 0], first_landed[unit, 0])
+        arrived(second_in.at[piece], second_landed[unit])
 
         @pl.loop(low_slot, high_slot)
         def _(tap):
@@ -789,11 +804,11 @@
                 else:
                     last_out[k - 1, tap] = total.astype(jnp.bfloat16)
 
-        piece = pl.ds(low_slot, high_slot - low_slot)
-        third_copies[unit] = [
-            send(last_out.at[k - 1, piece], last_in.at[k - 1, piece], z_peers[k - 1])
-            for k in range(1, n_q)
-        ]
+        for k in range(1, n_q):
+            send(
+                last_out.at[k - 1, piece], last_in.at[k - 1, piece], z_peers[k - 1],
+                third_sent, third_landed,
+            )
 
     def input_piece(index):
         total = None
@@ -818,8 +833,7 @@
 
     units = [(0, 3, width), (3, 5, half), (5, 7, half), (7, 9, half)]
     weight_tap(0)
-    for copy in side_edges[1]:
-        copy.wait_recv()
+    arrived(fields.at[0, pl.ds(0, 2)], edge_landed[1])
     weight_tap(1)
     reduce_tap(0, width)
     weight_tap(2)
@@ -833,8 +847,7 @@
 
     old.line_cross()
     old.line_step(1, ("own",))
-    for copy in x_halo:
-        copy.wait_recv()
+    x_halo.wait_recv()
 
     @pl.when(inner)
     def _():
@@ -870,35 +883,33 @@
                 chunk, group_rows, width
             )
 
-    side_edges[0], side_edges[2] = edges(0), edges(2)
-    old.line_step(1, ("x", "y"))
-    old.line_step(2, ("own",))
+    edges(0)
+    edges(2)
+    old.line_step(1, ("xy",))
     weight_tap(3)
     weight_tap(4)
     reduce_second(units[0])
     reduce_tap(3, half)
     reduce_tap(4, half)
     reduce_first(units[1])
-    old.line_far()
-    old.line_step(2, ("x", "y"))
-    old.line_step(3, ("own",))
-    for copy in side_edges[0] + side_edges[2]:
-        copy.wait_recv()
+    arrived(fields.at[0, pl.ds(0, 4)], edge_landed[0])
     weight_tap(5)
     weight_tap(6)
     reduce_tap(5, half)
     reduce_tap(6, half)
     reduce_first(units[2])
-    old.line_step(1, ("d",))
-    old.line_step(3, ("x", "y"))
+    old.line_far()
+    old.line_step(2, ("own",))
     weight_tap(7)
     weight_tap(8)
     reduce_tap(7, half)
     reduce_tap(8, half)
     reduce_first(units[3])
-    old.line_step(2, ("d",))
+    old.line_step(2, ("xy",))
+    old.line_step(1, ("d",))
     reduce_second(units[1])
     reduce_third(units[0])
+    old.line_step(3, ("own",))
     reduce_second(units[2])
     reduce_third(units[1])
     reduce_second(units[3])
@@ -910,15 +921,12 @@
         old.spread_x(k)
     reduce_third(units[2])
     reduce_third(units[3])
+    old.line_step(3, ("xy",))
+    old.line_step(2, ("d",))
     for k in range(n_q):
         old.relay_y(k)
         old.relay_x(k)
-    old.line_step(3, ("d",))
-    for step in range(4, n_q):
-        old.line_step(step)
-    for unit in units:
-        for copy in third_copies[unit]:
-            copy.wait_recv()
+    arrived(last_in, third_landed)
     square = jnp.zeros((rows, width), jnp.float32)
     for index, tap in enumerate(order):
         grad = mine[index, q]
@@ -928,22 +936,15 @@
         square = square + grad * grad
     square = jnp.sum(square)
     slot = 0
-    fill = [chunks // 2, chunks // 6]
-    done = 0
     for stage, peers in enumerate(([partner] + z_peers + z_twins, [x_peer, y_peer, d_peer])):
         norm_out[stage] = jnp.full(norm_out.shape[1:], square, jnp.float32)
-        copies = []
+        tiles = norm_in.at[pl.ds(slot, len(peers))]
+        sent, landed_at = outgoing(tiles), landing()
         for index, target in enumerate(peers):
-            copies.append(send(norm_out.at[stage], norm_in.at[slot + index], target))
-        if stage == 0:
-            for k in range(n_q):
-                old.close(k)
-            old.finish()
-        input_pieces(done, done + fill[stage])
-        done += fill[stage]
+            send(norm_out.at[stage], norm_in.at[slot + index], target, sent, landed_at)
+        arrived(tiles, landed_at)
         tile = norm_out[stage]
-        for index, copy in enumerate(copies):
-            copy.wait_recv()
+        for index in range(len(peers)):
             tile = tile + norm_in[slot + index]
         slot += len(peers)
         square = jnp.max(tile)
@@ -975,9 +976,17 @@
     new.spread_x(0)
     new.spread_y(0)
     new.core_copy(lat, 0, 0, width)
-    input_pieces(done, chunks)
+    old.line_step(3, ("d",))
+    for step in range(4, n_q):
+        old.line_step(step)
+    for k in range(n_q):
+        old.close(k)
+    old.finish()
+    cuts = [chunks * index // (n_q + 2) for index in range(n_q + 3)]
+    input_pieces(cuts[0], cuts[1])
     new.line_cross()
     for k in range(1, n_q):
+        input_pieces(cuts[k], cuts[k + 1])
         new.from_z(k)
         new.spread_x(k)
         new.spread_y(k)
@@ -986,35 +995,25 @@
         new.relay_y(k - 1)
         if k == 1:
             new.line_far()
-        new.line_step(k)
+        new.line_step(k - 1 if k > 1 else n_q)
+    input_pieces(cuts[n_q], cuts[n_q + 1])
     new.relay_x(n_q - 1)
     new.relay_y(n_q - 1)
+    new.line_step(n_q - 1)
+    input_pieces(cuts[n_q + 1], cuts[n_q + 2])
     for k in range(n_q):
         new.close(k)
     new.finish()
 
-    for copy in x_halo:
-        copy.wait_send()
-
-    @pl.when(inner)
-    def _():
-        y_halo.wait_send()
-        d_halo.wait_send()
-
-    @pl.when(outer)
-    def _():
-        passed.wait_send()
-
-    @pl.loop(0, taps)
-    def _(tap):
-        part_copy(tap).wait_send()
-
-    for copy in pending:
-        copy.wait_send()
-    for condition, copy in guarded:
-        @pl.when(condition)
-        def _(copy=copy):
+    for condition, copy in closing:
+        if condition is None:
             copy.wait_send()
+        else:
+            @pl.when(condition)
+            def _(copy=copy):
+                copy.wait_send()
+
+    assert used == [send_sem.shape[0], recv_sem.shape[0]]
 
 
 def land(*refs):
@@ -1058,7 +1057,7 @@
     lat_block = (taps, n_q, rows, width)
     vmem, hbm = (pl.BlockSpec(memory_space=m) for m in (pltpu.VMEM, pltpu.HBM))
     peers = 2 * n_q + n_lat - 2
-    copies = 192 + 32 * (n_q + n_lat)
+    sends, arrivals = 28 + 4 * (n_q - 1), 38 + 9 * n_q + 12 * (n_q - 1)
     return pl.pallas_call(
         functools.partial(whole_step, n_lat, n_q, max_norm),
         out_shape=(
@@ -1091,8 +1090,8 @@
             pltpu.VMEM((3, 8, LANE_TILE), f32),
             pltpu.VMEM((peers, 8, LANE_TILE), f32),
             pltpu.SemaphoreType.DMA((2 * batch + 3,)),
-            pltpu.SemaphoreType.DMA((copies,)),
-            pltpu.SemaphoreType.DMA((copies,)),
+            pltpu.SemaphoreType.DMA((sends,)),
+            pltpu.SemaphoreType.DMA((arrivals,)),
         ],
         compiler_params=pltpu.CompilerParams(
             collective_id=2, has_side_effects=True, vmem_limit_bytes=48 * 1024 * 1024

time: 105 us -> 90.7 us (0.86)
  Pallas kernels: 104 us -> 89.7 us
    pallas_call x1, Pallas kernels: 101 us -> 86.6 us  [fused_step(): pl.pallas_call(functools.partial(whole_step, n_lat, n_q, max_norm), out_s...]
where the time goes in v3:
time: 90.7 us; the launch traced here: 90.5 us
  Pallas kernels  89.7 us (99%)
    pallas_call x1, Pallas kernels, fused_step(): pl.pallas_call(functools.partial(whole_step, n_lat, n_q, max_norm), out_s...  86.6 us
    pallas_call x1, Pallas kernels, landed(): pl.pallas_call(land, out_shape=tuple((jax.ShapeDtypeStruct(a.shape, a.dty...  3.07 us

profile of v3, /device:TPU:0, one launch (start us, length us, event | category | flops | bytes accessed | tf_op | source)
XLA Modules:
  0.0 90.5 jit_solution(5949948346829021366)
XLA Ops:
  0.6 86.6 %whole_step.1 = (bf16[4,90,4,512]{3,2,1,0:T(4,128)(2,1)S(1)}, bf16[9,4,4,2,16,512]{5,4,3,2,1,0:T(8,128)(2,1)S(1)}, f32[9,16,512]{2,1,0:T(8,128)S(1)}, f32[9,16,5...) custom-call(bf16[4,90,4,512]{3,2,1,0:T(4,128)(2,1)} %bitcast.13, ...), custom_call_target="tpu_custom_call" | custom-call | tf_op jit(solution)/shard_map/whole_step/pallas_call | solution.py:1061
  87.3 3.1 %land.1 = (bf16[4,90,4,512]{3,2,1,0:T(4,128)(2,1)}, bf16[9,4,4,2,16,512]{5,4,3,2,1,0:T(8,128)(2,1)}, f32[9,16,512]{2,1,0:T(8,128)}, f32[9,16,512]{2,1,0:T(8,128)...) custom-call(bf16[4,90,4,512]{3,2,1,0:T(4,128)(2,1)S(1)} %get-tuple-element.18.refs_0_, ...), custom_call_target="tpu_custom_call" | custom-call | tf_op jit(solution)/shard_map/land/pallas_call | solution.py:1034

commit v4 on v3

--- a/solution.py
+++ b/solution.py
@@ -353,7 +353,7 @@
 
 LANE_TILE = 128
 ROW_TILE = 16
-OLD_LINE_TAPS = 6
+OLD_LINE_TAPS = 5
 NEW_LINE_TAPS = 2
 
 
@@ -847,21 +847,6 @@
 
     old.line_cross()
     old.line_step(1, ("own",))
-    x_halo.wait_recv()
-
-    @pl.when(inner)
-    def _():
-        d_halo.wait_recv()
-        passed.wait_recv()
-
-    @pl.when(jnp.logical_not(has_below))
-    def _():
-        halo_in[0] = jnp.zeros(halo_in.shape[1:], halo_in.dtype)
-
-    @pl.when(jnp.logical_not(has_above))
-    def _():
-        halo_in[1] = jnp.zeros(halo_in.shape[1:], halo_in.dtype)
-
     shift = [
         selector((span, span), lambda m, n: jnp.logical_and(n == m + 1, jnp.logical_not(last_row(m)))),
         selector((span, span), lambda m, n: jnp.logical_and(n == m - 1, jnp.logical_not(first_row(m)))),
@@ -876,10 +861,32 @@
         block = fields[1, pl.ds(1 + c * chunk, chunk)].reshape(span, width)
         for side in range(2):
             moved = jnp.dot(shift[side], block, preferred_element_type=jnp.float32)
-            moved = moved + jnp.dot(
-                place[side], halo_in[side, c], preferred_element_type=jnp.float32
+            fields[2 * side, pl.ds(1 + c * chunk, chunk)] = moved.astype(jnp.bfloat16).reshape(
+                chunk, group_rows, width
             )
-            fields[2 * side, pl.ds(1 + c * chunk, chunk)] = moved.astype(jnp.bfloat16).reshape(
+
+    x_halo.wait_recv()
+
+    @pl.when(inner)
+    def _():
+        d_halo.wait_recv()
+        passed.wait_recv()
+
+    @pl.when(jnp.logical_not(has_below))
+    def _():
+        halo_in[0] = jnp.zeros(halo_in.shape[1:], halo_in.dtype)
+
+    @pl.when(jnp.logical_not(has_above))
+    def _():
+        halo_in[1] = jnp.zeros(halo_in.shape[1:], halo_in.dtype)
+
+    @pl.loop(0, chunks)
+    def _(c):
+        for side in range(2):
+            piece = pl.ds(1 + c * chunk, chunk)
+            placed = jnp.dot(place[side], halo_in[side, c], preferred_element_type=jnp.float32)
+            inside = fields[2 * side, piece].reshape(span, width).astype(jnp.float32)
+            fields[2 * side, piece] = (inside + placed).astype(jnp.bfloat16).reshape(
                 chunk, group_rows, width
             )
 
@@ -905,12 +912,12 @@
     reduce_tap(7, half)
     reduce_tap(8, half)
     reduce_first(units[3])
+    reduce_second(units[1])
+    reduce_third(units[0])
+    reduce_second(units[2])
     old.line_step(2, ("xy",))
     old.line_step(1, ("d",))
-    reduce_second(units[1])
-    reduce_third(units[0])
     old.line_step(3, ("own",))
-    reduce_second(units[2])
     reduce_third(units[1])
     reduce_second(units[3])
     for k in range(1, n_q):

time: 90.7 us -> 88.6 us (0.977)
  Pallas kernels: 89.7 us -> 87.7 us
    pallas_call x1, Pallas kernels: 86.6 us -> 84.6 us  [fused_step(): pl.pallas_call(functools.partial(whole_step, n_lat, n_q, max_norm), out_s...]
where the time goes in v4:
time: 88.6 us; the launch traced here: 88.5 us
  Pallas kernels  87.7 us (99%)
    pallas_call x1, Pallas kernels, fused_step(): pl.pallas_call(functools.partial(whole_step, n_lat, n_q, max_norm), out_s...  84.6 us
    pallas_call x1, Pallas kernels, landed(): pl.pallas_call(land, out_shape=tuple((jax.ShapeDtypeStruct(a.shape, a.dty...  3.07 us

profile of v4, /device:TPU:0, one launch (start us, length us, event | category | flops | bytes accessed | tf_op | source)
XLA Modules:
  0.0 88.5 jit_solution(1296267740130414102)
XLA Ops:
  0.6 84.6 %whole_step.1 = (bf16[4,90,4,512]{3,2,1,0:T(4,128)(2,1)S(1)}, bf16[9,4,4,2,16,512]{5,4,3,2,1,0:T(8,128)(2,1)S(1)}, f32[9,16,512]{2,1,0:T(8,128)S(1)}, f32[9,16,5...) custom-call(bf16[4,90,4,512]{3,2,1,0:T(4,128)(2,1)} %bitcast.13, ...), custom_call_target="tpu_custom_call" | custom-call | tf_op jit(solution)/shard_map/whole_step/pallas_call | solution.py:1068
  85.2 3.1 %land.1 = (bf16[4,90,4,512]{3,2,1,0:T(4,128)(2,1)}, bf16[9,4,4,2,16,512]{5,4,3,2,1,0:T(8,128)(2,1)}, f32[9,16,512]{2,1,0:T(8,128)}, f32[9,16,512]{2,1,0:T(8,128)...) custom-call(bf16[4,90,4,512]{3,2,1,0:T(4,128)(2,1)S(1)} %get-tuple-element.18.refs_0_, ...), custom_call_target="tpu_custom_call" | custom-call | tf_op jit(solution)/shard_map/land/pallas_call | solution.py:1041
